TPU v7x, 32 devices: a 4x4x1 block of a 4x4x8 slice. The times are simulated.
32 devices in a mesh: dp: 1 (over z), tp: 4 (over y), ep: 8 (over x, core).
Axes of the slice: x: 4, y: 4, z: 1, core: 2. Of those that a mesh axis runs over, the one named last changes fastest.
The devices are a block of a 4x4x8 slice.
Arguments:
- tokens_in: bfloat16 [1024, 2048], P(('dp', 'ep', 'tp'))
- expert_ids: int32 [1024, 8], P(('dp', 'ep', 'tp'))
- router_gates: float32 [1024, 8], P(('dp', 'ep', 'tp'))
- w_gate: bfloat16 [64, 2048, 1024], P('ep', None, 'tp')
- w_up: bfloat16 [64, 2048, 1024], P('ep', None, 'tp')
- w_down: bfloat16 [64, 1024, 2048], P('ep', 'tp')
Outputs:
- output: bfloat16 [1024, 2048], P(('dp', 'ep', 'tp'))
All inputs are finite; a program needn't handle non-finite values.
Results may differ from a plain program's by a relative error of at most 0.00124.
Values are sent between devices in bfloat16 or wider.
A program may use at most 768 MiB of HBM per device.

v0:
```python
import jax
import jax.numpy as jnp
from jax import lax
from jax.sharding import PartitionSpec as P

TOKEN_AXES = ('dp', 'ep', 'tp')
GROUP_AXES = ('ep', 'tp')


def solution(mesh):
    groups = mesh.shape['ep']

    def expert_block(tok_shard, id_shard, gate_shard, w_gate, w_up, w_down):
        tok_group = lax.all_gather(tok_shard, GROUP_AXES, axis=0, tiled=True)
        id_group = lax.all_gather(id_shard, GROUP_AXES, axis=0, tiled=True)
        gate_group = lax.all_gather(gate_shard, GROUP_AXES, axis=0, tiled=True)
        tok_count, choices = id_group.shape
        local_count = w_gate.shape[0]
        pair_slots = tok_count * choices // groups
        local_exp = id_group.reshape(-1) - lax.axis_index('ep') * local_count
        sort_key = jnp.where((local_exp >= 0) & (local_exp < local_count), local_exp, local_count)
        sort_order = jnp.argsort(sort_key, stable=True)[:pair_slots]
        group_sizes = jnp.bincount(sort_key, length=local_count + 1)[:local_count].astype(jnp.int32)
        row_ids = sort_order // choices
        is_local = sort_key[sort_order] < local_count
        gate_rows = gate_group.reshape(-1)[sort_order]
        tok_rows = tok_group[row_ids]
        h_gate = lax.ragged_dot(tok_rows, w_gate, group_sizes, preferred_element_type=jnp.float32)
        h_up = lax.ragged_dot(tok_rows, w_up, group_sizes, preferred_element_type=jnp.float32)
        hidden = (jax.nn.silu(h_gate) * h_up).astype(jnp.bfloat16)
        out_rows = lax.ragged_dot(hidden, w_down, group_sizes, preferred_element_type=jnp.float32)
        weighted = jnp.where(is_local[:, None], out_rows * gate_rows[:, None], 0.0)
        partial_out = jax.ops.segment_sum(weighted, row_ids, num_segments=tok_count)
        y_shard = lax.psum_scatter(partial_out, GROUP_AXES, scatter_dimension=0, tiled=True)
        return y_shard.astype(jnp.bfloat16)

    return jax.shard_map(
        expert_block,
        mesh=mesh,
        in_specs=(P(TOKEN_AXES, None), P(TOKEN_AXES, None), P(TOKEN_AXES, None),
                  P('ep', None, 'tp'), P('ep', None, 'tp'), P('ep', 'tp', None)),
        out_specs=P(TOKEN_AXES, None),
        check_vma=False,
    )
```

profile of v0, /device:TPU:97, one launch (start us, length us, event | category | flops | bytes accessed | tf_op | source)
XLA Modules:
  0.0 324.3 jit_solution(13101670992418087981)
XLA Ops:
  6.6 0.7 all-gather.4.cloned.1.call-update
  7.3 0.1 reduce-scatter.2.cloned.1.call-start
  7.4 32.5 %all-gather = s32[32,32,8]{1,2,0:T(8,128)S(1)} all-gather(s32[1,32,8]{1,2,0:T(8,128)} %bitcast.5), channel_id=1, replica_groups=mesh['dp'=1,'tp'=4,'ep'=8] {'ep','tp'}, dimensions={0}, use_global_device_ids=true | all-gather | bytes 33792 | tf_op jit(solution)/shard_map/all_gather | solution.py:15
  39.9 0.2 copy.10
  40.1 0.3 sub.29
  40.4 0.3 sub.27
  40.7 0.1 fusion.3
  40.7 57.5 %scatter_custom_fusion = s32[9]{0:T(128)} fusion(s32[8192]{0:T(1024)S(1)} %bitcast.4, s32[8192]{0:T(1024)S(1)} %broadcast.74, s32[]{:T(128)} %constant.14.clone.1), kind=kCustom, calls=%fused_computation.26 | custom fusion | flops 8192 | bytes 40 | tf_op jit(solution)/shard_map/scatter-add | solution.py:23
  98.2 1.5 ragged-dot-metadata
  99.8 6.8 %sort.17 = (s32[8192]{0:T(1024)}, s32[8192]{0:T(1024)S(1)}) sort(s32[8192]{0:T(1024)S(1)} %and_select_fusion.1, s32[8192]{0:T(1024)S(1)} %iota.4), dimensions={0}, to_apply=%region_0.1 | sort | flops 106496 | bytes 131072 | tf_op jit(solution)/shard_map/jit(argsort)/sort | solution.py:22
  106.6 6.2 %gather_fusion = s32[1024]{0:T(1024)S(1)} fusion(s32[8192]{0:T(1024)S(1)} %and_select_fusion.1, s32[1024]{0:T(1024)S(1)} %get-tuple-element.19), kind=kCustom, calls=%fused_computation | custom fusion | bytes 12288 | tf_op jit(solution)/shard_map/gather | solution.py:25
  112.7 33.2 %all-gather.1 = f32[32,32,8]{1,2,0:T(8,128)S(1)} all-gather(f32[1,32,8]{1,2,0:T(8,128)} %bitcast.6), channel_id=1, replica_groups=mesh['dp'=1,'tp'=4,'ep'=8] {'ep','tp'}, dimensions={0}, use_global_device_ids=true | all-gather | bytes 33792 | tf_op jit(solution)/shard_map/all_gather | solution.py:16
  145.9 0.2 copy.12
  146.2 0.3 reshape.37
  146.4 6.2 %gather_fusion.2 = f32[1024]{0:T(1024)S(1)} fusion(f32[8192]{0:T(1024)S(1)} %reshape.37, s32[1024]{0:T(1024)S(1)} %get-tuple-element.19), kind=kCustom, calls=%fused_computation.2 | custom fusion | bytes 12288 | tf_op jit(solution)/shard_map/gather | solution.py:26
  152.6 11.6 %gather_fusion.1 = bf16[1024,2048]{1,0:T(8,128)(2,1)} fusion(bf16[1024,2048]{1,0:T(8,128)(2,1)} %all-gather.4.cloned.1.call-done, s32[1024]{0:T(1024)S(1)} %get-tuple-element.20), kind=kCustom, calls=%fused_computation.1 | custom fusion | bytes 8392704 | tf_op jit(solution)/shard_map/gather | solution.py:27
  164.2 12.7 %ragged-dot-none.2 = f32[1024,256]{1,0:T(8,128)} custom-call(s32[1]{0:T(128)} %get-tuple-element.7, s32[9]{0:T(128)} %get-tuple-element.8, s32[11]{0:T(128)} %get-tuple-element.9, s32[11]{0:T(128)} %get-tuple-element.10, s32[1]{0:T(128)} %get-tuple-element.7, bf16[1024,2048]{1,0:T(8,128)(2,1)} %gather_fusion.1, bf16[8,2048,256]{2,1,0:T(8,128)(2,1)} %param.9), custom_call_target="tpu_custom_call" | custom-call | flops 1073741824 | bytes 13631520 | tf_op jit(solution)/shard_map/ragged_dot_general/ragged-dot-none
  176.9 12.8 %ragged-dot-none.1 = f32[1024,256]{1,0:T(8,128)} custom-call(s32[1]{0:T(128)} %get-tuple-element.7, s32[9]{0:T(128)} %get-tuple-element.8, s32[11]{0:T(128)} %get-tuple-element.9, s32[11]{0:T(128)} %get-tuple-element.10, s32[1]{0:T(128)} %get-tuple-element.7, bf16[1024,2048]{1,0:T(8,128)(2,1)} %gather_fusion.1, bf16[8,2048,256]{2,1,0:T(8,128)(2,1)} %param.10), custom_call_target="tpu_custom_call" | custom-call | flops 1073741824 | bytes 13631520 | tf_op jit(solution)/shard_map/ragged_dot_general/ragged-dot-none
  189.7 2.4 multiply_convert_fusion
  192.0 14.1 %ragged-dot-none = f32[1024,2048]{1,0:T(8,128)} custom-call(s32[1]{0:T(128)} %get-tuple-element.7, s32[9]{0:T(128)} %get-tuple-element.8, s32[11]{0:T(128)} %get-tuple-element.9, s32[11]{0:T(128)} %get-tuple-element.10, s32[1]{0:T(128)} %get-tuple-element.7, bf16[1024,256]{1,0:T(8,128)(2,1)} %multiply_convert_fusion, bf16[8,256,2048]{2,1,0:T(8,128)(2,1)} %param.11), custom_call_target="tpu_custom_call" | custom-call | flops 1073741824 | bytes 17301536 | tf_op jit(solution)/shard_map/ragged_dot_general/ragged-dot-none
  206.2 19.3 %scatter_custom_fusion.1 = f32[1024,2048]{1,0:T(8,128)} fusion(s32[1024]{0:T(1024)S(1)} %get-tuple-element.21, f32[1024,2048]{1,0:T(8,128)} %ragged-dot-none, f32[1024]{0:T(1024)S(1)} %gather_fusion.2, f32[]{:T(128)} %constant.11.clone.1, pred[1024]{0:T(1024)(128)(4,1)S(1)} %broadcast_compare_fusion), kind=kCustom, calls=%fused_computation.6 | custom fusion | flops 6291456 | bytes 16783360 | tf_op jit(solution)/shard_map/scatter-add | solution.py:33
  225.4 0.1 reduce-scatter.2.cloned.1.call-update
  225.5 90.4 %reduce-scatter.2.cloned.1.call-done = f32[32,2048]{1,0:T(8,128)} async-done(((f32[1024,2048]{1,0:T(8,128)}), f32[32,2048]{1,0:T(8,128)}) %reduce-scatter.2.cloned.1.call-update) | async-done | bytes 262160 | tf_op jit(solution)/shard_map/reduce_scatter | solution.py:34
  315.9 1.6 convert_element_type.7
  (10 shorter events, 0.1 us)
Async XLA Ops:
  6.5 146.1 %all-gather.4.cloned.1.call-start = ((), (), s32[]{:S(2)}) async-start(), calls=%async_computation.1 | async-start | bytes 4325376 | tf_op jit(solution)/shard_map/all_gather | solution.py:14
  7.3 308.6 %reduce-scatter.2.cloned.1.call-start = ((), (), s32[]{:S(2)}) async-start(), calls=%async_computation.2 | async-start | bytes 8650752 | tf_op jit(solution)/shard_map/reduce_scatter | solution.py:34
  176.9 12.8 %copy-start = (f32[1024,256]{1,0:T(8,128)S(1)}, f32[1024,256]{1,0:T(8,128)}, u32[]{:S(2)}) copy-start(f32[1024,256]{1,0:T(8,128)} %ragged-dot-none.2) | copy-start | bytes 3145732
Sparse Core Ops, SparseCore 0:
  9.4 45.1 all-gather.3
  225.6 90.2 reduce-scatter.1
where the time goes:
time: 326 us; the launch traced here: 324 us
  waiting for transfers between devices  91.2 us (28%)
  other arithmetic  87.6 us (27%)
  blocking collectives  65.7 us (20%)
  Pallas kernels  41.1 us (13%)
  local copies, waits for them, and re-layouts  25.1 us (8%)
  between operations  13.5 us (4%)
    reduce_scatter x1, waiting for transfers between devices, expert_block(): lax.psum_scatter(partial_out, GROUP_AXES, scatter_dimension=0, tiled=True)  90.4 us
    scatter-add x1, other arithmetic, expert_block(): jnp.bincount(sort_key, length=local_count + 1)[:local_count]  57.5 us
    another operation x3, Pallas kernels  39.6 us
    all_gather x1, blocking collectives, expert_block(): gate_group = lax.all_gather(gate_shard, GROUP_AXES, axis=0, tiled=True)  33.2 us
    all_gather x1, blocking collectives, expert_block(): id_group = lax.all_gather(id_shard, GROUP_AXES, axis=0, tiled=True)  32.5 us
    scatter-add x1, other arithmetic, expert_block(): partial_out = jax.ops.segment_sum(weighted, row_ids, num_segments=tok_count)  19.3 us
    gather x1, local copies, waits for them, and re-layouts, expert_block(): tok_rows = tok_group[row_ids]  11.6 us
    sort x1, other arithmetic, expert_block(): sort_order = jnp.argsort(sort_key, stable=True)[:pair_slots]  6.77 us
  transfers between devices with their start and end apart: 2, of which 1 were waited for; matrix products, arithmetic and copies ran while one was open for 24% of the time, Pallas kernels for 0%

commit v1 on v0

v1 whole, which is shorter than its diff:
```python
import functools

import jax
import jax.numpy as jnp
from jax import lax
from jax.experimental import pallas as pl
from jax.experimental.pallas import tpu as pltpu
from jax.sharding import PartitionSpec as P

TOKEN_AXES = ('dp', 'ep', 'tp')
LANES = 128
F32 = jnp.float32
BF16 = jnp.bfloat16


def split3(v):
    hi = v.astype(BF16)
    rest = v - hi.astype(F32)
    mid = rest.astype(BF16)
    low = (rest - mid.astype(F32)).astype(BF16)
    return hi, mid, low


def dot(a, b):
    return lax.dot_general(a, b, (((1,), (0,)), ((), ())), preferred_element_type=F32)


def dot_nt(a, b):
    return lax.dot_general(a, b, (((1,), (1,)), ((), ())), preferred_element_type=F32)


def moe_kernel(names, ep_n, tp_n, tok_hbm, ids_hbm, gate_hbm, wg_hbm, wu_hbm, wd_hbm, out_ref,
               wg, wu, wd, xg, idg, gg, xs, gs, xr, gr, acc_g, acc_u, hb, gb, ob, zr, yb, yr, slot_of, row_of,
               w_sem, in_sem, ag_ss, ag_rs, id_ss, id_rs, dx_ss, dx_rs, dg_ss, dg_rs, cx_ss, cx_rs, cy_ss, cy_rs):
    rows, d = tok_hbm.shape
    local = wg_hbm.shape[0]
    choices = ids_hbm.shape[1]
    shard_rows = rows * tp_n
    cap = 2 * shard_rows // ep_n
    slots = cap * ep_n
    kcs = 4
    kw = d // kcs

    ep = lax.axis_index('ep')
    tp = lax.axis_index('tp')

    def device(ep_i, tp_i):
        at = {'dp': lax.axis_index('dp'), 'ep': ep_i, 'tp': tp_i}
        return tuple(at[n] for n in names)

    chips = ep_n // 2
    x_peers = [(dx, cf) for dx in (2, 1, chips - 1, 0) for cf in (0, 1) if (dx, cf) != (0, 0)]

    def x_target(p):
        return lax.rem(ep // 2 + p[0], chips) * 2 + lax.rem(ep + p[1], 2)

    def y_target(dt):
        return lax.rem(tp + dt, tp_n)

    def rdma(src, dst, ss, rs, dev):
        return pltpu.make_async_remote_copy(src_ref=src, dst_ref=dst, send_sem=ss, recv_sem=rs,
                                            device_id=dev, device_id_type=pl.DeviceIdType.MESH)

    my_rows = pl.ds(pl.multiple_of(tp * rows, rows), rows)
    my_slots = pl.ds(pl.multiple_of(ep * cap, cap), cap)

    own = [pltpu.make_async_copy(ids_hbm, idg.at[my_rows], in_sem.at[0]),
           pltpu.make_async_copy(gate_hbm, gg.at[my_rows], in_sem.at[1]),
           pltpu.make_async_copy(tok_hbm, xg.at[my_rows], in_sem.at[2])]
    for c in own:
        c.start()

    bar = pltpu.get_barrier_semaphore()
    for dt in range(1, tp_n):
        pl.semaphore_signal(bar, inc=1, device_id=device(ep, y_target(dt)), device_id_type=pl.DeviceIdType.MESH)
    for p in x_peers:
        pl.semaphore_signal(bar, inc=1, device_id=device(x_target(p), tp), device_id_type=pl.DeviceIdType.MESH)
    loads = []
    for i, (src, dst) in enumerate(((wg_hbm, wg), (wu_hbm, wu), (wd_hbm, wd))):
        for e in range(local):
            loads.append(pltpu.make_async_copy(src.at[e], dst.at[e], w_sem.at[i, e]))
    for c in own:
        c.wait()
    pl.semaphore_wait(bar, tp_n - 1 + len(x_peers))

    id_cps, ag_cps = [], []
    for dt in range(1, tp_n):
        dev = device(ep, y_target(dt))
        id_cps.append(rdma(idg.at[my_rows], idg.at[my_rows], id_ss.at[0, dt - 1], id_rs.at[0, dt - 1], dev))
        id_cps.append(rdma(gg.at[my_rows], gg.at[my_rows], id_ss.at[1, dt - 1], id_rs.at[1, dt - 1], dev))
    for kc in range(kcs):
        for dt in (2, 1, 3):
            dev = device(ep, y_target(dt))
            part = xg.at[my_rows, pl.ds(kc * kw, kw)]
            ag_cps.append(rdma(part, part, ag_ss.at[kc, dt - 1], ag_rs.at[kc, dt - 1], dev))
    for c in id_cps + ag_cps:
        c.start()
    for c in loads:
        c.start()
    for c in id_cps:
        c.wait_recv()

    lane = lax.broadcasted_iota(jnp.int32, (shard_rows, LANES), 1)
    used = jnp.zeros((shard_rows, LANES), jnp.bool_)
    gate_of = jnp.zeros((shard_rows, LANES), F32)
    ids = idg[...]
    gates = gg[...]
    for j in range(choices):
        e_j = ids[:, j:j + 1]
        used = used | (e_j // local == lane)
        gate_of = gate_of + jnp.where(e_j == lane, gates[:, j:j + 1], 0.0)
    used_b = used.astype(F32).astype(BF16)
    before = (lax.broadcasted_iota(jnp.int32, (shard_rows, shard_rows), 0)
              > lax.broadcasted_iota(jnp.int32, (shard_rows, shard_rows), 1)).astype(F32).astype(BF16)
    rank = dot(before, used_b).astype(BF16)
    s_iota = lax.broadcasted_iota(jnp.int32, (slots, LANES), 0)
    expand = (s_iota // cap == lax.broadcasted_iota(jnp.int32, (slots, LANES), 1)).astype(F32).astype(BF16)
    in_slot = lax.broadcasted_iota(jnp.int32, (slots, shard_rows), 0) % cap
    s1 = (dot_nt(expand, used_b) > 0.5) & (dot_nt(expand, rank) == in_slot.astype(F32))
    slot_of[...] = s1.astype(F32).astype(BF16)
    in_slot_t = lax.broadcasted_iota(jnp.int32, (shard_rows, slots), 1) % cap
    s2 = (dot_nt(used_b, expand) > 0.5) & (dot_nt(rank, expand) == in_slot_t.astype(F32))
    row_of[...] = s2.astype(F32).astype(BF16)

    dx_cps, dg_cps = [], []
    for kc in range(kcs):
        cols = pl.ds(kc * kw, kw)
        for dt in range(1, tp_n):
            ag_cps[kc * (tp_n - 1) + {2: 0, 1: 1, 3: 2}[dt]].wait_recv()
        xs[:, cols] = dot(slot_of[...], xg[:, cols]).astype(BF16)
        for i, p in enumerate(x_peers):
            to = x_target(p)
            src = xs.at[pl.ds(pl.multiple_of(to * cap, cap), cap), cols]
            c = rdma(src, xr.at[my_slots, cols], dx_ss.at[kc, i], dx_rs.at[kc, i], device(to, tp))
            c.start()
            dx_cps.append(c)
        xr[my_slots, cols] = xs[my_slots, cols]
        if kc == 0:
            g1, g2, g3 = split3(gate_of)
            gs[...] = dot(slot_of[...], g1) + dot(slot_of[...], g2) + dot(slot_of[...], g3)
            gr[my_slots, :] = gs[my_slots, :]
            for i, p in enumerate(x_peers):
                to = x_target(p)
                src = gs.at[pl.ds(pl.multiple_of(to * cap, cap), cap)]
                c = rdma(src, gr.at[my_slots], dg_ss.at[i], dg_rs.at[i], device(to, tp))
                c.start()
                dg_cps.append(c)

    for c in loads:
        c.wait()
    g_lane = lax.broadcasted_iota(jnp.int32, (slots, LANES), 1)
    for kc in range(kcs):
        cols = pl.ds(kc * kw, kw)
        for i in range(len(x_peers)):
            dx_cps[kc * len(x_peers) + i].wait_recv()
        if kc == 0:
            for c in dg_cps:
                c.wait_recv()

            def spread(e, carry):
                col = jnp.sum(jnp.where(g_lane == ep * local + e, gr[...], 0.0), axis=1, keepdims=True)
                gb[e] = jnp.broadcast_to(col, (slots, LANES))
                return carry

            lax.fori_loop(0, local, spread, 0)

        def up(e, carry, kc=kc, cols=cols):
            x = xr[:, cols]
            a = dot(x, wg[e, cols, :])
            b = dot(x, wu[e, cols, :])
            if kc > 0:
                a = a + acc_g[e]
                b = b + acc_u[e]
            if kc < kcs - 1:
                acc_g[e] = a
                acc_u[e] = b
            else:
                h = a * jax.nn.sigmoid(a) * b
                g = gb[e]
                on = jnp.concatenate([g] * (h.shape[1] // LANES), axis=1) > 0.0
                hb[e] = jnp.where(on, h, 0.0).astype(BF16)
            return carry

        lax.fori_loop(0, local, up, 0)

    cx_cps, cy_cps = [], []
    for kc in range(kcs):
        cols = pl.ds(kc * kw, kw)

        def down(e, carry, cols=cols):
            g = gb[e]
            o = dot(hb[e], wd[e, :, cols]) * jnp.concatenate([g] * (kw // LANES), axis=1)

            @pl.when(e == 0)
            def _():
                ob[:, cols] = o

            @pl.when(e > 0)
            def _():
                ob[:, cols] = ob[:, cols] + o

            return carry

        lax.fori_loop(0, local, down, 0)
        for i, p in enumerate(x_peers):
            to = x_target(p)
            src = ob.at[pl.ds(pl.multiple_of(to * cap, cap), cap), cols]
            c = rdma(src, zr.at[my_slots, cols], cx_ss.at[kc, i], cx_rs.at[kc, i], device(to, tp))
            c.start()
            cx_cps.append(c)
        zr[my_slots, cols] = ob[my_slots, cols]

    for kc in range(kcs):
        cols = pl.ds(kc * kw, kw)
        for i in range(len(x_peers)):
            cx_cps[kc * len(x_peers) + i].wait_recv()
        z1, z2, z3 = split3(zr[:, cols])
        pick = row_of[...]
        yb[:, cols] = dot(pick, z3) + dot(pick, z2) + dot(pick, z1)
        for dt in (2, 1, 3):
            to = y_target(dt)
            src = yb.at[pl.ds(pl.multiple_of(to * rows, rows), rows), cols]
            c = rdma(src, yr.at[dt - 1, :, cols], cy_ss.at[kc, dt - 1], cy_rs.at[kc, dt - 1], device(ep, to))
            c.start()
            cy_cps.append(c)
    for kc in range(kcs):
        cols = pl.ds(kc * kw, kw)
        for i in range(tp_n - 1):
            cy_cps[kc * (tp_n - 1) + i].wait_recv()
        total = yb[my_rows, cols]
        for i in range(tp_n - 1):
            total = total + yr[i, :, cols]
        out_ref[:, cols] = total.astype(BF16)

    for c in id_cps + ag_cps + dx_cps + dg_cps + cx_cps + cy_cps:
        c.wait_send()


def solution(mesh):
    ep_n = mesh.shape['ep']
    tp_n = mesh.shape['tp']
    names = tuple(mesh.axis_names)

    def block(tok, ids, gates, w_gate, w_up, w_down):
        rows, d = tok.shape
        local, _, hid = w_gate.shape
        shard_rows = rows * tp_n
        slots = 2 * shard_rows
        kcs = 4
        nx = ep_n - 1
        ny = tp_n - 1
        any_spec = pl.BlockSpec(memory_space=pl.ANY)
        dma = pltpu.SemaphoreType.DMA
        return pl.pallas_call(
            functools.partial(moe_kernel, names, ep_n, tp_n),
            out_shape=jax.ShapeDtypeStruct((rows, d), BF16),
            in_specs=[any_spec] * 6,
            out_specs=pl.BlockSpec(memory_space=pltpu.VMEM),
            scratch_shapes=[
                pltpu.VMEM((local, d, hid), BF16),
                pltpu.VMEM((local, d, hid), BF16),
                pltpu.VMEM((local, hid, d), BF16),
                pltpu.VMEM((shard_rows, d), BF16),
                pltpu.VMEM((shard_rows, ids.shape[1]), jnp.int32),
                pltpu.VMEM((shard_rows, gates.shape[1]), F32),
                pltpu.VMEM((slots, d), BF16),
                pltpu.VMEM((slots, LANES), F32),
                pltpu.VMEM((slots, d), BF16),
                pltpu.VMEM((slots, LANES), F32),
                pltpu.VMEM((local, slots, hid), F32),
                pltpu.VMEM((local, slots, hid), F32),
                pltpu.VMEM((local, slots, hid), BF16),
                pltpu.VMEM((local, slots, LANES), F32),
                pltpu.VMEM((slots, d), F32),
                pltpu.VMEM((slots, d), F32),
                pltpu.VMEM((shard_rows, d), F32),
                pltpu.VMEM((ny, rows, d), F32),
                pltpu.VMEM((slots, shard_rows), BF16),
                pltpu.VMEM((shard_rows, slots), BF16),
                dma((3, local)), dma((3,)),
                dma((kcs, ny)), dma((kcs, ny)),
                dma((2, ny)), dma((2, ny)),
                dma((kcs, nx)), dma((kcs, nx)),
                dma((nx,)), dma((nx,)),
                dma((kcs, nx)), dma((kcs, nx)),
                dma((kcs, ny)), dma((kcs, ny)),
            ],
            compiler_params=pltpu.CompilerParams(collective_id=0, has_side_effects=True,
                                                 vmem_limit_bytes=60 * 1024 * 1024),
        )(tok, ids, gates, w_gate, w_up, w_down)

    return jax.shard_map(
        block,
        mesh=mesh,
        in_specs=(P(TOKEN_AXES, None), P(TOKEN_AXES, None), P(TOKEN_AXES, None),
                  P('ep', None, 'tp'), P('ep', None, 'tp'), P('ep', 'tp', None)),
        out_specs=P(TOKEN_AXES, None),
        check_vma=False,
    )
```

time: 326 us -> 70.7 us (0.22)
  waiting for transfers between devices: 91.2 us -> 0 us
  other arithmetic: 87.6 us -> 0 us
  blocking collectives: 65.7 us -> 0 us
  Pallas kernels: 41.1 us -> 66.2 us
  local copies, waits for them, and re-layouts: 25.1 us -> 4.29 us
  between operations: 13.5 us -> 0.01 us
    reduce_scatter x1 -> x0, waiting for transfers between devices: 90.4 us -> none  [expert_block(): lax.psum_scatter(partial_out, GROUP_AXES, scatter_dimension=0, tiled=True)]
    scatter-add x2 -> x0, other arithmetic: 76.8 us -> none  [the longest x1 57.5 us: expert_block(): jnp.bincount(sort_key, length=local_count + 1)[:local_count]]
    pallas_call x0 -> x1, Pallas kernels: none -> 66.2 us  [block(): pl.pallas_call(functools.partial(moe_kernel, names, ep_n, tp_n), out_shap...]
    all_gather x2 -> x0, blocking collectives: 65.7 us -> none  [the longest x1 33.2 us: expert_block(): gate_group = lax.all_gather(gate_shard, GROUP_AXES, axis=0, tiled=True)]
    another operation x3 -> x0, Pallas kernels: 39.6 us -> none
    gather x3 -> x0, local copies, waits for them, and re-layouts: 23.9 us -> none  [the longest x1 11.6 us: expert_block(): tok_rows = tok_group[row_ids]]
    sort x1 -> x0, other arithmetic: 6.77 us -> none  [expert_block(): sort_order = jnp.argsort(sort_key, stable=True)[:pair_slots]]
    unnamed x2 -> x3, local copies, waits for them, and re-layouts: 0.01 us -> 4.29 us
  transfers between devices with their start and end apart: 2 -> 0, of which waited for: 1 -> 0; matrix products, arithmetic and copies ran while one was open for 24% -> 0% of each run, Pallas kernels for 0% -> 0%
where the time goes in v1:
time: 70.7 us; the launch traced here: 70.5 us
  Pallas kernels  66.2 us (94%)
  local copies, waits for them, and re-layouts  4.29 us (6%)
    pallas_call x1, Pallas kernels, block(): pl.pallas_call(functools.partial(moe_kernel, names, ep_n, tp_n), out_shap...  66.2 us
    unnamed x3, local copies, waits for them, and re-layouts  4.29 us

profile of v1, /device:TPU:97, one launch (start us, length us, event | category | flops | bytes accessed | tf_op | source)
XLA Modules:
  0.0 70.5 jit_solution(3691416659778358315)
XLA Ops:
  0.0 1.4 %copy.7.ids_hbm = s32[32,8]{1,0:T(8,128)} copy(s32[32,8]{0,1:T(8,128)} %param.7) | data formatting | bytes 2048 | tf_op args[1]
  1.4 1.4 %copy.8.gate_hbm = f32[32,8]{1,0:T(8,128)} copy(f32[32,8]{0,1:T(8,128)} %param.8) | data formatting | bytes 2048 | tf_op args[2]
  2.7 66.2 %shard_map.64 = bf16[32,2048]{1,0:T(8,128)(2,1)} custom-call(bf16[32,2048]{1,0:T(8,128)(2,1)} %tok_hbm.1, s32[32,8]{1,0:T(8,128)} %copy.7.ids_hbm, f32[32,8]{1,0:T(8,128)} %copy.8.gate_hbm, bf16[8,2048,256]{2,1,0:T(8,128)(2,1)} %wg_hbm.1, bf16[8,2048,256]{2,1,0:T(8,128)(2,1)} %wu_hbm.1, bf16[8,256,2048]{2,1,0:T(8,128)(2,1)} %wd_hbm.1), custom_call_target="tpu_custom_call" | custom-call | tf_op jit(solution)/shard_map/pallas_call | solution.py:254
  68.9 1.6 %copy.10 = bf16[32,2048]{1,0:T(8,128)(2,1)} copy(bf16[32,2048]{1,0:T(8,128)(2,1)} %shard_map.64) | data formatting | bytes 262144

commit v2 on v1

--- a/solution.py
+++ b/solution.py
@@ -30,14 +30,15 @@
 
 
 def moe_kernel(names, ep_n, tp_n, tok_hbm, ids_hbm, gate_hbm, wg_hbm, wu_hbm, wd_hbm, out_ref,
-               wg, wu, wd, xg, idg, gg, xs, gs, xr, gr, acc_g, acc_u, hb, gb, ob, zr, yb, yr, slot_of, row_of,
+               wg, wu, wd, xg, idg, gg, xs, gs, xr, gr, acc_g, acc_u, hb, gb, ob, zr, yb, yr, slot_of, row_of, gcols,
                w_sem, in_sem, ag_ss, ag_rs, id_ss, id_rs, dx_ss, dx_rs, dg_ss, dg_rs, cx_ss, cx_rs, cy_ss, cy_rs):
     rows, d = tok_hbm.shape
     local = wg_hbm.shape[0]
-    choices = ids_hbm.shape[1]
+    choices = ids_hbm.shape[0]
     shard_rows = rows * tp_n
     cap = 2 * shard_rows // ep_n
     slots = cap * ep_n
+    per_tile = LANES // cap
     kcs = 4
     kw = d // kcs
 
@@ -64,8 +65,8 @@
     my_rows = pl.ds(pl.multiple_of(tp * rows, rows), rows)
     my_slots = pl.ds(pl.multiple_of(ep * cap, cap), cap)
 
-    own = [pltpu.make_async_copy(ids_hbm, idg.at[my_rows], in_sem.at[0]),
-           pltpu.make_async_copy(gate_hbm, gg.at[my_rows], in_sem.at[1]),
+    own = [pltpu.make_async_copy(ids_hbm, idg.at[tp], in_sem.at[0]),
+           pltpu.make_async_copy(gate_hbm, gg.at[tp], in_sem.at[1]),
            pltpu.make_async_copy(tok_hbm, xg.at[my_rows], in_sem.at[2])]
     for c in own:
         c.start()
@@ -86,8 +87,8 @@
     id_cps, ag_cps = [], []
     for dt in range(1, tp_n):
         dev = device(ep, y_target(dt))
-        id_cps.append(rdma(idg.at[my_rows], idg.at[my_rows], id_ss.at[0, dt - 1], id_rs.at[0, dt - 1], dev))
-        id_cps.append(rdma(gg.at[my_rows], gg.at[my_rows], id_ss.at[1, dt - 1], id_rs.at[1, dt - 1], dev))
+        id_cps.append(rdma(idg.at[tp], idg.at[tp], id_ss.at[0, dt - 1], id_rs.at[0, dt - 1], dev))
+        id_cps.append(rdma(gg.at[tp], gg.at[tp], id_ss.at[1, dt - 1], id_rs.at[1, dt - 1], dev))
     for kc in range(kcs):
         for dt in (2, 1, 3):
             dev = device(ep, y_target(dt))
@@ -100,27 +101,20 @@
     for c in id_cps:
         c.wait_recv()
 
-    lane = lax.broadcasted_iota(jnp.int32, (shard_rows, LANES), 1)
-    used = jnp.zeros((shard_rows, LANES), jnp.bool_)
-    gate_of = jnp.zeros((shard_rows, LANES), F32)
-    ids = idg[...]
-    gates = gg[...]
+    ids = jnp.concatenate([idg[q] for q in range(tp_n)], axis=1)
+    gates = jnp.concatenate([gg[q] for q in range(tp_n)], axis=1)
+    b_iota = lax.broadcasted_iota(jnp.int32, (ep_n, shard_rows), 0)
+    used = jnp.zeros((ep_n, shard_rows), F32)
     for j in range(choices):
-        e_j = ids[:, j:j + 1]
-        used = used | (e_j // local == lane)
-        gate_of = gate_of + jnp.where(e_j == lane, gates[:, j:j + 1], 0.0)
-    used_b = used.astype(F32).astype(BF16)
+        used = jnp.where(ids[j:j + 1, :] // local == b_iota, 1.0, used)
     before = (lax.broadcasted_iota(jnp.int32, (shard_rows, shard_rows), 0)
-              > lax.broadcasted_iota(jnp.int32, (shard_rows, shard_rows), 1)).astype(F32).astype(BF16)
-    rank = dot(before, used_b).astype(BF16)
-    s_iota = lax.broadcasted_iota(jnp.int32, (slots, LANES), 0)
-    expand = (s_iota // cap == lax.broadcasted_iota(jnp.int32, (slots, LANES), 1)).astype(F32).astype(BF16)
-    in_slot = lax.broadcasted_iota(jnp.int32, (slots, shard_rows), 0) % cap
-    s1 = (dot_nt(expand, used_b) > 0.5) & (dot_nt(expand, rank) == in_slot.astype(F32))
-    slot_of[...] = s1.astype(F32).astype(BF16)
-    in_slot_t = lax.broadcasted_iota(jnp.int32, (shard_rows, slots), 1) % cap
-    s2 = (dot_nt(used_b, expand) > 0.5) & (dot_nt(rank, expand) == in_slot_t.astype(F32))
-    row_of[...] = s2.astype(F32).astype(BF16)
+              < lax.broadcasted_iota(jnp.int32, (shard_rows, shard_rows), 1)).astype(F32).astype(BF16)
+    rank = dot(used.astype(BF16), before)
+    place = jnp.where(used > 0.0, rank, -1.0)
+    in_slot = lax.broadcasted_iota(jnp.int32, (cap, shard_rows), 0).astype(F32)
+    for b in range(ep_n):
+        hit = jnp.where(place[b:b + 1, :] == in_slot, 1.0, 0.0)
+        slot_of[pl.ds(b * cap, cap), :] = hit.astype(BF16)
 
     dx_cps, dg_cps = [], []
     for kc in range(kcs):
@@ -136,19 +130,27 @@
             dx_cps.append(c)
         xr[my_slots, cols] = xs[my_slots, cols]
         if kc == 0:
+            e_iota = lax.broadcasted_iota(jnp.int32, (ep_n * local, shard_rows), 0)
+            gate_of = jnp.zeros((ep_n * local, shard_rows), F32)
+            for j in range(choices):
+                gate_of = jnp.where(ids[j:j + 1, :] == e_iota, gates[j:j + 1, :], gate_of)
             g1, g2, g3 = split3(gate_of)
-            gs[...] = dot(slot_of[...], g1) + dot(slot_of[...], g2) + dot(slot_of[...], g3)
-            gr[my_slots, :] = gs[my_slots, :]
+            gs[...] = dot_nt(g3, slot_of[...]) + dot_nt(g2, slot_of[...]) + dot_nt(g1, slot_of[...])
+
+            def gate_tile(b):
+                return (pl.ds(pl.multiple_of(b * local, local), local),
+                        pl.ds(pl.multiple_of(b // per_tile * LANES, LANES), LANES))
+
             for i, p in enumerate(x_peers):
                 to = x_target(p)
-                src = gs.at[pl.ds(pl.multiple_of(to * cap, cap), cap)]
-                c = rdma(src, gr.at[my_slots], dg_ss.at[i], dg_rs.at[i], device(to, tp))
+                c = rdma(gs.at[gate_tile(to)], gr.at[ep], dg_ss.at[i], dg_rs.at[i], device(to, tp))
                 c.start()
                 dg_cps.append(c)
+            gr[ep] = gs[gate_tile(ep)]
+    row_of[...] = jnp.transpose(slot_of[...].astype(F32)).astype(BF16)
 
     for c in loads:
         c.wait()
-    g_lane = lax.broadcasted_iota(jnp.int32, (slots, LANES), 1)
     for kc in range(kcs):
         cols = pl.ds(kc * kw, kw)
         for i in range(len(x_peers)):
@@ -157,12 +159,12 @@
             for c in dg_cps:
                 c.wait_recv()
 
-            def spread(e, carry):
-                col = jnp.sum(jnp.where(g_lane == ep * local + e, gr[...], 0.0), axis=1, keepdims=True)
-                gb[e] = jnp.broadcast_to(col, (slots, LANES))
-                return carry
-
-            lax.fori_loop(0, local, spread, 0)
+            lanes_of_mine = pl.ds(pl.multiple_of(lax.rem(ep, per_tile) * cap, cap), cap)
+            for a in range(ep_n):
+                gcols[...] = jnp.transpose(jnp.concatenate([gr[a]] * (LANES // local), axis=0))
+                cols_a = gcols[lanes_of_mine, :]
+                for e in range(local):
+                    gb[e, pl.ds(a * cap, cap), :] = jnp.broadcast_to(cols_a[:, e:e + 1], (cap, LANES))
 
         def up(e, carry, kc=kc, cols=cols):
             x = xr[:, cols]
@@ -181,27 +183,17 @@
                 hb[e] = jnp.where(on, h, 0.0).astype(BF16)
             return carry
 
-        lax.fori_loop(0, local, up, 0)
+        lax.fori_loop(0, local, up, 0, unroll=True)
 
     cx_cps, cy_cps = [], []
     for kc in range(kcs):
         cols = pl.ds(kc * kw, kw)
 
-        def down(e, carry, cols=cols):
-            g = gb[e]
-            o = dot(hb[e], wd[e, :, cols]) * jnp.concatenate([g] * (kw // LANES), axis=1)
-
-            @pl.when(e == 0)
-            def _():
-                ob[:, cols] = o
-
-            @pl.when(e > 0)
-            def _():
-                ob[:, cols] = ob[:, cols] + o
-
-            return carry
-
-        lax.fori_loop(0, local, down, 0)
+        total = None
+        for e in range(local):
+            o = dot(hb[e], wd[e, :, cols]) * jnp.concatenate([gb[e]] * (kw // LANES), axis=1)
+            total = o if total is None else total + o
+        ob[:, cols] = total
         for i, p in enumerate(x_peers):
             to = x_target(p)
             src = ob.at[pl.ds(pl.multiple_of(to * cap, cap), cap), cols]
@@ -253,7 +245,7 @@
         dma = pltpu.SemaphoreType.DMA
         return pl.pallas_call(
             functools.partial(moe_kernel, names, ep_n, tp_n),
-            out_shape=jax.ShapeDtypeStruct((rows, d), BF16),
+            out_shape=pltpu.VMEM((rows, d), BF16),
             in_specs=[any_spec] * 6,
             out_specs=pl.BlockSpec(memory_space=pltpu.VMEM),
             scratch_shapes=[
@@ -261,12 +253,12 @@
                 pltpu.VMEM((local, d, hid), BF16),
                 pltpu.VMEM((local, hid, d), BF16),
                 pltpu.VMEM((shard_rows, d), BF16),
-                pltpu.VMEM((shard_rows, ids.shape[1]), jnp.int32),
-                pltpu.VMEM((shard_rows, gates.shape[1]), F32),
+                pltpu.VMEM((tp_n, ids.shape[1], rows), jnp.int32),
+                pltpu.VMEM((tp_n, gates.shape[1], rows), F32),
                 pltpu.VMEM((slots, d), BF16),
-                pltpu.VMEM((slots, LANES), F32),
+                pltpu.VMEM((ep_n * local, slots), F32),
                 pltpu.VMEM((slots, d), BF16),
-                pltpu.VMEM((slots, LANES), F32),
+                pltpu.VMEM((ep_n, local, LANES), F32),
                 pltpu.VMEM((local, slots, hid), F32),
                 pltpu.VMEM((local, slots, hid), F32),
                 pltpu.VMEM((local, slots, hid), BF16),
@@ -277,6 +269,7 @@
                 pltpu.VMEM((ny, rows, d), F32),
                 pltpu.VMEM((slots, shard_rows), BF16),
                 pltpu.VMEM((shard_rows, slots), BF16),
+                pltpu.VMEM((LANES, LANES), F32),
                 dma((3, local)), dma((3,)),
                 dma((kcs, ny)), dma((kcs, ny)),
                 dma((2, ny)), dma((2, ny)),
@@ -287,7 +280,7 @@
             ],
             compiler_params=pltpu.CompilerParams(collective_id=0, has_side_effects=True,
                                                  vmem_limit_bytes=60 * 1024 * 1024),
-        )(tok, ids, gates, w_gate, w_up, w_down)
+        )(tok, ids.T, gates.T, w_gate, w_up, w_down)
 
     return jax.shard_map(
         block,

time: 70.7 us -> 58.3 us (0.82)
  Pallas kernels: 66.2 us -> 57.6 us
  local copies, waits for them, and re-layouts: 4.29 us -> 0.66 us
    pallas_call x1, Pallas kernels: 66.2 us -> 57.6 us  [block(): pl.pallas_call(functools.partial(moe_kernel, names, ep_n, tp_n), out_shap...]
    unnamed x3 -> x1, local copies, waits for them, and re-layouts: 4.29 us -> 0.66 us
where the time goes in v2:
time: 58.3 us; the launch traced here: 58.2 us
  Pallas kernels  57.6 us (99%)
  local copies, waits for them, and re-layouts  0.66 us (1%)
    pallas_call x1, Pallas kernels, block(): pl.pallas_call(functools.partial(moe_kernel, names, ep_n, tp_n), out_shap...  57.6 us

profile of v2, /device:TPU:97, one launch (start us, length us, event | category | flops | bytes accessed | tf_op | source)
XLA Modules:
  0.0 58.2 jit_solution(11232032729201634385)
XLA Ops:
  0.0 57.6 %shard_map.64 = bf16[32,2048]{1,0:T(8,128)(2,1)S(1)} custom-call(bf16[32,2048]{1,0:T(8,128)(2,1)} %tok_hbm.1, s32[8,32]{1,0:T(8,128)} %bitcast.2, f32[8,32]{1,0:T(8,128)} %bitcast.3, bf16[8,2048,256]{2,1,0:T(8,128)(2,1)} %wg_hbm.1, bf16[8,2048,256]{2,1,0:T(8,128)(2,1)} %wu_hbm.1, bf16[8,256,2048]{2,1,0:T(8,128)(2,1)} %wd_hbm.1), custom_call_target="tpu_custom_call" | custom-call | tf_op jit(solution)/shard_map/pallas_call | solution.py:246
  57.6 0.7 %copy.8 = bf16[32,2048]{1,0:T(8,128)(2,1)} copy(bf16[32,2048]{1,0:T(8,128)(2,1)S(1)} %shard_map.64) | data formatting | bytes 262144

commit v3 on v2

--- a/solution.py
+++ b/solution.py
@@ -30,8 +30,8 @@
 
 
 def moe_kernel(names, ep_n, tp_n, tok_hbm, ids_hbm, gate_hbm, wg_hbm, wu_hbm, wd_hbm, out_ref,
-               wg, wu, wd, xg, idg, gg, xs, gs, xr, gr, acc_g, acc_u, hb, gb, ob, zr, yb, yr, slot_of, row_of, gcols,
-               w_sem, in_sem, ag_ss, ag_rs, id_ss, id_rs, dx_ss, dx_rs, dg_ss, dg_rs, cx_ss, cx_rs, cy_ss, cy_rs):
+               wg, wu, wd, xg, idg, gg, xs, gs, xr, gr, acc_g, acc_u, hb, gb, ob, zr, yb, yr, yf, zs, slot_of, row_of, gcols,
+               w_sem, in_sem, ag_ss, ag_rs, id_ss, id_rs, dx_ss, dx_rs, dg_ss, dg_rs, cx_ss, cx_rs, yf_ss, yf_rs, zf_ss, zf_rs, cy_ss, cy_rs):
     rows, d = tok_hbm.shape
     local = wg_hbm.shape[0]
     choices = ids_hbm.shape[0]
@@ -52,6 +52,10 @@
     chips = ep_n // 2
     x_peers = [(dx, cf) for dx in (2, 1, chips - 1, 0) for cf in (0, 1) if (dx, cf) != (0, 0)]
 
+    far = [p for p in x_peers if 2 * p[0] == chips]
+    near = [p for p in x_peers if 2 * p[0] != chips]
+    qw = kw // tp_n
+
     def x_target(p):
         return lax.rem(ep // 2 + p[0], chips) * 2 + lax.rem(ep + p[1], 2)
 
@@ -64,12 +68,21 @@
 
     my_rows = pl.ds(pl.multiple_of(tp * rows, rows), rows)
     my_slots = pl.ds(pl.multiple_of(ep * cap, cap), cap)
+
+    def slots_of(e):
+        return pl.ds(pl.multiple_of(e * cap, cap), cap)
+
+    def quarter(kc, t):
+        return pl.ds(pl.multiple_of(kc * kw + t * qw, qw), qw)
 
     own = [pltpu.make_async_copy(ids_hbm, idg.at[tp], in_sem.at[0]),
            pltpu.make_async_copy(gate_hbm, gg.at[tp], in_sem.at[1]),
            pltpu.make_async_copy(tok_hbm, xg.at[my_rows], in_sem.at[2])]
     for c in own:
         c.start()
+
+    for p in far:
+        zr[slots_of(x_target(p)), :] = jnp.zeros((cap, d), F32)
 
     bar = pltpu.get_barrier_semaphore()
     for dt in range(1, tp_n):
@@ -185,27 +198,62 @@
 
         lax.fori_loop(0, local, up, 0, unroll=True)
 
-    cx_cps, cy_cps = [], []
-    for kc in range(kcs):
-        cols = pl.ds(kc * kw, kw)
-
+    cx_cps, yf_cps, zf_cps, cy_cps = [], [], [], []
+
+    def down(kc):
+        cols = pl.ds(kc * kw, kw)
         total = None
         for e in range(local):
             o = dot(hb[e], wd[e, :, cols]) * jnp.concatenate([gb[e]] * (kw // LANES), axis=1)
             total = o if total is None else total + o
         ob[:, cols] = total
-        for i, p in enumerate(x_peers):
+        zr[my_slots, cols] = ob[my_slots, cols]
+        for j, p in enumerate(far):
+            for dt in (2, 1, 3):
+                q = y_target(dt)
+                c = rdma(ob.at[slots_of(x_target(p)), quarter(kc, q)], yf.at[dt - 1, j, :, pl.ds(kc * qw, qw)],
+                         yf_ss.at[kc, j, dt - 1], yf_rs.at[kc, j, dt - 1], device(ep, q))
+                c.start()
+                yf_cps.append(c)
+
+    def send_near(kc):
+        cols = pl.ds(kc * kw, kw)
+        for i, p in enumerate(near):
             to = x_target(p)
-            src = ob.at[pl.ds(pl.multiple_of(to * cap, cap), cap), cols]
-            c = rdma(src, zr.at[my_slots, cols], cx_ss.at[kc, i], cx_rs.at[kc, i], device(to, tp))
+            c = rdma(ob.at[slots_of(to), cols], zr.at[my_slots, cols], cx_ss.at[kc, i], cx_rs.at[kc, i], device(to, tp))
             c.start()
             cx_cps.append(c)
-        zr[my_slots, cols] = ob[my_slots, cols]
-
-    for kc in range(kcs):
-        cols = pl.ds(kc * kw, kw)
-        for i in range(len(x_peers)):
-            cx_cps[kc * len(x_peers) + i].wait_recv()
+
+    def send_far(kc):
+        part = pl.ds(kc * qw, qw)
+        per = len(far) * (tp_n - 1)
+        for c in yf_cps[kc * per:(kc + 1) * per]:
+            c.wait_recv()
+        for j, p in enumerate(far):
+            to = x_target(p)
+            total = ob[slots_of(to), quarter(kc, tp)]
+            for i in range(tp_n - 1):
+                total = total + yf[i, j, :, part]
+            zs[j, :, part] = total
+            c = rdma(zs.at[j, :, part], zr.at[my_slots, quarter(kc, tp)], zf_ss.at[kc, j], zf_rs.at[kc, j],
+                     device(to, tp))
+            c.start()
+            zf_cps.append(c)
+
+    lead = kcs // 2
+    for kc in range(kcs):
+        down(kc)
+        if kc < lead:
+            send_near(kc)
+    for kc in range(kcs):
+        send_far(kc)
+        if kc + lead < kcs:
+            send_near(kc + lead)
+
+    for kc in range(kcs):
+        cols = pl.ds(kc * kw, kw)
+        for c in cx_cps[kc * len(near):(kc + 1) * len(near)] + zf_cps[kc * len(far):(kc + 1) * len(far)]:
+            c.wait_recv()
         z1, z2, z3 = split3(zr[:, cols])
         pick = row_of[...]
         yb[:, cols] = dot(pick, z3) + dot(pick, z2) + dot(pick, z1)
@@ -224,7 +272,7 @@
             total = total + yr[i, :, cols]
         out_ref[:, cols] = total.astype(BF16)
 
-    for c in id_cps + ag_cps + dx_cps + dg_cps + cx_cps + cy_cps:
+    for c in id_cps + ag_cps + dx_cps + dg_cps + cx_cps + yf_cps + zf_cps + cy_cps:
         c.wait_send()
 
 
@@ -267,6 +315,8 @@
                 pltpu.VMEM((slots, d), F32),
                 pltpu.VMEM((shard_rows, d), F32),
                 pltpu.VMEM((ny, rows, d), F32),
+                pltpu.VMEM((ny, 2, slots // ep_n, d // tp_n), F32),
+                pltpu.VMEM((2, slots // ep_n, d // tp_n), F32),
                 pltpu.VMEM((slots, shard_rows), BF16),
                 pltpu.VMEM((shard_rows, slots), BF16),
                 pltpu.VMEM((LANES, LANES), F32),
@@ -275,7 +325,9 @@
                 dma((2, ny)), dma((2, ny)),
                 dma((kcs, nx)), dma((kcs, nx)),
                 dma((nx,)), dma((nx,)),
-                dma((kcs, nx)), dma((kcs, nx)),
+                dma((kcs, nx - 2)), dma((kcs, nx - 2)),
+                dma((kcs, 2, ny)), dma((kcs, 2, ny)),
+                dma((kcs, 2)), dma((kcs, 2)),
                 dma((kcs, ny)), dma((kcs, ny)),
             ],
             compiler_params=pltpu.CompilerParams(collective_id=0, has_side_effects=True,

time: 58.3 us -> 53.2 us (0.913)
  Pallas kernels: 57.6 us -> 52.2 us
    pallas_call x1, Pallas kernels: 57.6 us -> 52.2 us  [block(): pl.pallas_call(functools.partial(moe_kernel, names, ep_n, tp_n), out_shap...]
where the time goes in v3:
time: 53.2 us; the launch traced here: 52.9 us
  Pallas kernels  52.2 us (98%)
  local copies, waits for them, and re-layouts  0.66 us (1%)
    pallas_call x1, Pallas kernels, block(): pl.pallas_call(functools.partial(moe_kernel, names, ep_n, tp_n), out_shap...  52.2 us

profile of v3, /device:TPU:97, one launch (start us, length us, event | category | flops | bytes accessed | tf_op | source)
XLA Modules:
  0.0 52.9 jit_solution(14006834077031543407)
XLA Ops:
  0.0 52.2 %shard_map.64 = bf16[32,2048]{1,0:T(8,128)(2,1)S(1)} custom-call(bf16[32,2048]{1,0:T(8,128)(2,1)} %tok_hbm.1, s32[8,32]{1,0:T(8,128)} %bitcast.2, f32[8,32]{1,0:T(8,128)} %bitcast.3, bf16[8,2048,256]{2,1,0:T(8,128)(2,1)} %wg_hbm.1, bf16[8,2048,256]{2,1,0:T(8,128)(2,1)} %wu_hbm.1, bf16[8,256,2048]{2,1,0:T(8,128)(2,1)} %wd_hbm.1), custom_call_target="tpu_custom_call" | custom-call | tf_op jit(solution)/shard_map/pallas_call | solution.py:294
  52.2 0.7 %copy.8 = bf16[32,2048]{1,0:T(8,128)(2,1)} copy(bf16[32,2048]{1,0:T(8,128)(2,1)S(1)} %shard_map.64) | data formatting | bytes 262144

commit v4 on v3

--- a/solution.py
+++ b/solution.py
@@ -31,7 +31,7 @@
 
 def moe_kernel(names, ep_n, tp_n, tok_hbm, ids_hbm, gate_hbm, wg_hbm, wu_hbm, wd_hbm, out_ref,
                wg, wu, wd, xg, idg, gg, xs, gs, xr, gr, acc_g, acc_u, hb, gb, ob, zr, yb, yr, yf, zs, slot_of, row_of, gcols,
-               w_sem, in_sem, ag_ss, ag_rs, id_ss, id_rs, dx_ss, dx_rs, dg_ss, dg_rs, cx_ss, cx_rs, yf_ss, yf_rs, zf_ss, zf_rs, cy_ss, cy_rs):
+               w_sem, in_sem, ag_ss, ag_rs, id_ss, id_rs, dx_ss, dx_rs, dg_ss, dg_rs, df_ss, df_rs, dq_ss, dq_rs, cx_ss, cx_rs, yf_ss, yf_rs, zf_ss, zf_rs, cy_ss, cy_rs):
     rows, d = tok_hbm.shape
     local = wg_hbm.shape[0]
     choices = ids_hbm.shape[0]
@@ -71,6 +71,13 @@
 
     def slots_of(e):
         return pl.ds(pl.multiple_of(e * cap, cap), cap)
+
+    turns = (0, 1, tp_n - 1, 2)
+    far_chip = lax.rem(ep // 2 + chips // 2, chips)
+    far_slots = pl.ds(pl.multiple_of(far_chip * (2 * cap), 2 * cap), 2 * cap)
+
+    def chunk(t):
+        return pl.ds(pl.multiple_of(t * kw, kw), kw)
 
     def quarter(kc, t):
         return pl.ds(pl.multiple_of(kc * kw + t * qw, qw), qw)
@@ -105,7 +112,7 @@
     for kc in range(kcs):
         for dt in (2, 1, 3):
             dev = device(ep, y_target(dt))
-            part = xg.at[my_rows, pl.ds(kc * kw, kw)]
+            part = xg.at[my_rows, chunk(y_target(dt + turns[kc]))]
             ag_cps.append(rdma(part, part, ag_ss.at[kc, dt - 1], ag_rs.at[kc, dt - 1], dev))
     for c in id_cps + ag_cps:
         c.start()
@@ -129,16 +136,21 @@
         hit = jnp.where(place[b:b + 1, :] == in_slot, 1.0, 0.0)
         slot_of[pl.ds(b * cap, cap), :] = hit.astype(BF16)
 
-    dx_cps, dg_cps = [], []
-    for kc in range(kcs):
-        cols = pl.ds(kc * kw, kw)
+    dx_cps, dg_cps, df_cps = [], [], []
+    for kc in range(kcs):
+        cols = chunk(y_target(turns[kc]))
         for dt in range(1, tp_n):
             ag_cps[kc * (tp_n - 1) + {2: 0, 1: 1, 3: 2}[dt]].wait_recv()
         xs[:, cols] = dot(slot_of[...], xg[:, cols]).astype(BF16)
-        for i, p in enumerate(x_peers):
+        if kc == 0:
+            for i, p in enumerate(far):
+                to = x_target(p)
+                c = rdma(xs.at[slots_of(to), cols], xr.at[my_slots, cols], df_ss.at[i], df_rs.at[i], device(to, tp))
+                c.start()
+                df_cps.append(c)
+        for i, p in enumerate(near):
             to = x_target(p)
-            src = xs.at[pl.ds(pl.multiple_of(to * cap, cap), cap), cols]
-            c = rdma(src, xr.at[my_slots, cols], dx_ss.at[kc, i], dx_rs.at[kc, i], device(to, tp))
+            c = rdma(xs.at[slots_of(to), cols], xr.at[my_slots, cols], dx_ss.at[kc, i], dx_rs.at[kc, i], device(to, tp))
             c.start()
             dx_cps.append(c)
         xr[my_slots, cols] = xs[my_slots, cols]
@@ -162,12 +174,21 @@
             gr[ep] = gs[gate_tile(ep)]
     row_of[...] = jnp.transpose(slot_of[...].astype(F32)).astype(BF16)
 
+    for c in df_cps:
+        c.wait_recv()
+    dq_cps = {}
+    for dt in (3, 1, 2):
+        part = xr.at[far_slots, chunk(tp)]
+        dq_cps[dt] = rdma(part, part, dq_ss.at[dt - 1], dq_rs.at[dt - 1], device(ep, y_target(dt)))
+        dq_cps[dt].start()
     for c in loads:
         c.wait()
     for kc in range(kcs):
-        cols = pl.ds(kc * kw, kw)
-        for i in range(len(x_peers)):
-            dx_cps[kc * len(x_peers) + i].wait_recv()
+        cols = chunk(y_target(turns[kc]))
+        for c in dx_cps[kc * len(near):(kc + 1) * len(near)]:
+            c.wait_recv()
+        if kc > 0:
+            dq_cps[tp_n - turns[kc]].wait_recv()
         if kc == 0:
             for c in dg_cps:
                 c.wait_recv()
@@ -272,7 +293,7 @@
             total = total + yr[i, :, cols]
         out_ref[:, cols] = total.astype(BF16)
 
-    for c in id_cps + ag_cps + dx_cps + dg_cps + cx_cps + yf_cps + zf_cps + cy_cps:
+    for c in id_cps + ag_cps + dx_cps + dg_cps + df_cps + list(dq_cps.values()) + cx_cps + yf_cps + zf_cps + cy_cps:
         c.wait_send()
 
 
@@ -323,8 +344,10 @@
                 dma((3, local)), dma((3,)),
                 dma((kcs, ny)), dma((kcs, ny)),
                 dma((2, ny)), dma((2, ny)),
-                dma((kcs, nx)), dma((kcs, nx)),
+                dma((kcs, nx - 2)), dma((kcs, nx - 2)),
                 dma((nx,)), dma((nx,)),
+                dma((2,)), dma((2,)),
+                dma((ny,)), dma((ny,)),
                 dma((kcs, nx - 2)), dma((kcs, nx - 2)),
                 dma((kcs, 2, ny)), dma((kcs, 2, ny)),
                 dma((kcs, 2)), dma((kcs, 2)),

time: 53.2 us -> 53.9 us (1.013)
  Pallas kernels: 52.2 us -> 53.2 us
    pallas_call x1, Pallas kernels: 52.2 us -> 53.2 us  [block(): pl.pallas_call(functools.partial(moe_kernel, names, ep_n, tp_n), out_shap...]
where the time goes in v4:
time: 53.9 us; the launch traced here: 53.8 us
  Pallas kernels  53.2 us (99%)
  local copies, waits for them, and re-layouts  0.66 us (1%)
    pallas_call x1, Pallas kernels, block(): pl.pallas_call(functools.partial(moe_kernel, names, ep_n, tp_n), out_shap...  53.2 us

profile of v4, /device:TPU:97, one launch (start us, length us, event | category | flops | bytes accessed | tf_op | source)
XLA Modules:
  0.0 53.8 jit_solution(10982092668391466802)
XLA Ops:
  0.0 53.2 %shard_map.64 = bf16[32,2048]{1,0:T(8,128)(2,1)S(1)} custom-call(bf16[32,2048]{1,0:T(8,128)(2,1)} %tok_hbm.1, s32[8,32]{1,0:T(8,128)} %bitcast.2, f32[8,32]{1,0:T(8,128)} %bitcast.3, bf16[8,2048,256]{2,1,0:T(8,128)(2,1)} %wg_hbm.1, bf16[8,2048,256]{2,1,0:T(8,128)(2,1)} %wu_hbm.1, bf16[8,256,2048]{2,1,0:T(8,128)(2,1)} %wd_hbm.1), custom_call_target="tpu_custom_call" | custom-call | tf_op jit(solution)/shard_map/pallas_call | solution.py:315
  53.2 0.7 %copy.8 = bf16[32,2048]{1,0:T(8,128)(2,1)} copy(bf16[32,2048]{1,0:T(8,128)(2,1)S(1)} %shard_map.64) | data formatting | bytes 262144

commit v5 on v2

v5 whole, which is shorter than its diff:
```python
import functools

import jax
import jax.numpy as jnp
from jax import lax
from jax.experimental import pallas as pl
from jax.experimental.pallas import tpu as pltpu
from jax.sharding import PartitionSpec as P

TOKEN_AXES = ('dp', 'ep', 'tp')
LANES = 128
CHUNKS = 4
F32 = jnp.float32
BF16 = jnp.bfloat16
MESH = pl.DeviceIdType.MESH


def split3(v):
    hi = v.astype(BF16)
    rest = v - hi.astype(F32)
    mid = rest.astype(BF16)
    low = (rest - mid.astype(F32)).astype(BF16)
    return hi, mid, low


def dot(a, b):
    return lax.dot_general(a, b, (((1,), (0,)), ((), ())), preferred_element_type=F32)


def dot_nt(a, b):
    return lax.dot_general(a, b, (((1,), (1,)), ((), ())), preferred_element_type=F32)


def arrived(ref, sem):
    pltpu.make_async_copy(ref, ref, sem).wait()


def moe_kernel(names, ep_n, tp_n, tok_hbm, ids_hbm, gate_hbm, wg_hbm, wu_hbm, wd_hbm, out_ref,
               wg, wu, wd, xg, idg, gg, xs, gs, xr, gr, acc_g, acc_u, hb, gb, ob, zr, yb, yr, yf, zs,
               slot_of, row_of, gcols,
               w_sem, in_sem, id_sem, ag_rs, dg_rs, df_rs, dx_rs, dq_rs, cx_rs, yf_rs, zf_rs, cy_rs, out_sem):
    rows, d = tok_hbm.shape
    local = wg_hbm.shape[0]
    choices = ids_hbm.shape[0]
    shard_rows = rows * tp_n
    cap = 2 * shard_rows // ep_n
    slots = cap * ep_n
    per_tile = LANES // cap
    kw = d // CHUNKS
    qw = kw // tp_n
    chips = ep_n // 2

    ep = lax.axis_index('ep')
    tp = lax.axis_index('tp')

    def device(ep_i, tp_i):
        at = {'dp': lax.axis_index('dp'), 'ep': ep_i, 'tp': tp_i}
        return tuple(at[n] for n in names)

    far = [(chips // 2, 0), (chips // 2, 1)]
    near = [(1, 0), (1, 1), (chips - 1, 0), (chips - 1, 1), (0, 1)]
    x_peers = far + near
    turns = (0, 1, tp_n - 1, 2)

    def x_target(p):
        return lax.rem(ep // 2 + p[0], chips) * 2 + lax.rem(ep + p[1], 2)

    def y_target(dt):
        return lax.rem(tp + dt, tp_n)

    def send(src, dst, ss, rs, dev):
        pltpu.make_async_remote_copy(src_ref=src, dst_ref=dst, send_sem=ss, recv_sem=rs,
                                     device_id=dev, device_id_type=MESH).start()

    def rows_at(i, n):
        return pl.ds(pl.multiple_of(i * n, n), n)

    def slots_of(e):
        return rows_at(e, cap)

    def chunk(t):
        return pl.ds(pl.multiple_of(t * kw, kw), kw)

    def quarter(kc, t):
        return pl.ds(pl.multiple_of(kc * kw + t * qw, qw), qw)

    my_rows = rows_at(tp, rows)
    my_slots = slots_of(ep)
    far_slots = rows_at(lax.rem(ep // 2 + chips // 2, chips), 2 * cap)
    near_rows = pl.ds(0, len(near) * cap)
    others = tp_n - 1

    own = [pltpu.make_async_copy(ids_hbm, idg.at[tp], in_sem.at[0]),
           pltpu.make_async_copy(gate_hbm, gg.at[tp], in_sem.at[1]),
           pltpu.make_async_copy(tok_hbm, xg.at[my_rows], in_sem.at[2])]
    for c in own:
        c.start()

    zr[far_slots, :] = jnp.zeros((2 * cap, d), F32)

    bar = pltpu.get_barrier_semaphore()
    for dt in range(1, tp_n):
        pl.semaphore_signal(bar, inc=1, device_id=device(ep, y_target(dt)), device_id_type=MESH)
    for p in x_peers:
        pl.semaphore_signal(bar, inc=1, device_id=device(x_target(p), tp), device_id_type=MESH)
    for c in own:
        c.wait()
    pl.semaphore_wait(bar, others + len(x_peers))

    for dt in range(1, tp_n):
        dev = device(ep, y_target(dt))
        send(idg.at[tp], idg.at[tp], id_sem.at[0], id_sem.at[1], dev)
        send(gg.at[tp], gg.at[tp], id_sem.at[2], id_sem.at[3], dev)
    for kc in range(CHUNKS):
        for dt in (2, 1, 3):
            part = xg.at[my_rows, chunk(y_target(dt + turns[kc]))]
            send(part, part, out_sem.at[0], ag_rs.at[kc], device(ep, y_target(dt)))
    for i, (src, dst) in enumerate(((wg_hbm, wg), (wu_hbm, wu), (wd_hbm, wd))):
        for e in range(local):
            pltpu.make_async_copy(src.at[e], dst.at[e], w_sem.at[i]).start()
    arrived(idg.at[pl.ds(0, others)], id_sem.at[1])
    arrived(gg.at[pl.ds(0, others)], id_sem.at[3])

    ids = jnp.concatenate([idg[q] for q in range(tp_n)], axis=1)
    gates = jnp.concatenate([gg[q] for q in range(tp_n)], axis=1)
    b_iota = lax.broadcasted_iota(jnp.int32, (ep_n, shard_rows), 0)
    used = jnp.zeros((ep_n, shard_rows), F32)
    for j in range(choices):
        used = jnp.where(ids[j:j + 1, :] // local == b_iota, 1.0, used)
    before = (lax.broadcasted_iota(jnp.int32, (shard_rows, shard_rows), 0)
              < lax.broadcasted_iota(jnp.int32, (shard_rows, shard_rows), 1)).astype(F32).astype(BF16)
    rank = dot(used.astype(BF16), before)
    place = jnp.where(used > 0.0, rank, -1.0)
    in_slot = lax.broadcasted_iota(jnp.int32, (cap, shard_rows), 0).astype(F32)
    for b in range(ep_n):
        hit = jnp.where(place[b:b + 1, :] == in_slot, 1.0, 0.0)
        slot_of[pl.ds(b * cap, cap), :] = hit.astype(BF16)

    e_iota = lax.broadcasted_iota(jnp.int32, (ep_n * local, shard_rows), 0)
    gate_of = jnp.zeros((ep_n * local, shard_rows), F32)
    for j in range(choices):
        gate_of = jnp.where(ids[j:j + 1, :] == e_iota, gates[j:j + 1, :], gate_of)
    g1, g2, g3 = split3(gate_of)
    gs[...] = dot_nt(g3, slot_of[...]) + dot_nt(g2, slot_of[...]) + dot_nt(g1, slot_of[...])

    def gate_tile(b):
        return (rows_at(b, local), rows_at(b // per_tile, LANES))

    for p in x_peers:
        to = x_target(p)
        send(gs.at[gate_tile(to)], gr.at[ep], out_sem.at[1], dg_rs.at[0], device(to, tp))
    gr[ep] = gs[gate_tile(ep)]

    for kc in range(CHUNKS):
        cols = chunk(y_target(turns[kc]))
        arrived(xg.at[pl.ds(0, others * rows), pl.ds(0, kw)], ag_rs.at[kc])
        xs[:, cols] = dot(slot_of[...], xg[:, cols]).astype(BF16)
        if kc == 0:
            for p in far:
                to = x_target(p)
                send(xs.at[slots_of(to), cols], xr.at[my_slots, cols], out_sem.at[2], df_rs.at[0], device(to, tp))
        for p in near:
            to = x_target(p)
            send(xs.at[slots_of(to), cols], xr.at[my_slots, cols], out_sem.at[3], dx_rs.at[kc], device(to, tp))
        xr[my_slots, cols] = xs[my_slots, cols]
    row_of[...] = jnp.transpose(slot_of[...].astype(F32)).astype(BF16)

    arrived(xs.at[pl.ds(0, 2 * cap), pl.ds(0, kw)], df_rs.at[0])
    for dt in (3, 1, 2):
        part = xr.at[far_slots, chunk(tp)]
        send(part, part, out_sem.at[4], dq_rs.at[dt - 1], device(ep, y_target(dt)))

    arrived(gr.at[pl.ds(0, len(x_peers))], dg_rs.at[0])
    lanes_of_mine = rows_at(lax.rem(ep, per_tile), cap)
    for a in range(ep_n):
        gcols[...] = jnp.transpose(jnp.concatenate([gr[a]] * (LANES // local), axis=0))
        cols_a = gcols[lanes_of_mine, :]
        for e in range(local):
            gb[e, pl.ds(a * cap, cap), :] = jnp.broadcast_to(cols_a[:, e:e + 1], (cap, LANES))

    arrived(wg, w_sem.at[0])
    arrived(wu, w_sem.at[1])
    for kc in range(CHUNKS):
        cols = chunk(y_target(turns[kc]))
        arrived(xr.at[near_rows, pl.ds(0, kw)], dx_rs.at[kc])
        if kc > 0:
            arrived(xr.at[pl.ds(0, 2 * cap), pl.ds(0, kw)], dq_rs.at[tp_n - turns[kc] - 1])

        def up(e, carry, kc=kc, cols=cols):
            x = xr[:, cols]
            a = dot(x, wg[e, cols, :])
            b = dot(x, wu[e, cols, :])
            if kc > 0:
                a = a + acc_g[e]
                b = b + acc_u[e]
            if kc < CHUNKS - 1:
                acc_g[e] = a
                acc_u[e] = b
            else:
                h = a * jax.nn.sigmoid(a) * b
                on = jnp.concatenate([gb[e]] * (h.shape[1] // LANES), axis=1) > 0.0
                hb[e] = jnp.where(on, h, 0.0).astype(BF16)
            return carry

        lax.fori_loop(0, local, up, 0, unroll=True)

    arrived(wd, w_sem.at[2])

    def down(kc):
        cols = pl.ds(kc * kw, kw)
        total = None
        for e in range(local):
            o = dot(hb[e], wd[e, :, cols]) * jnp.concatenate([gb[e]] * (kw // LANES), axis=1)
            total = o if total is None else total + o
        ob[:, cols] = total
        zr[my_slots, cols] = ob[my_slots, cols]
        for j, p in enumerate(far):
            for dt in (2, 1, 3):
                q = y_target(dt)
                send(ob.at[slots_of(x_target(p)), quarter(kc, q)], yf.at[dt - 1, j, :, pl.ds(kc * qw, qw)],
                     out_sem.at[5], yf_rs.at[kc], device(ep, q))

    def send_near(kc):
        cols = pl.ds(kc * kw, kw)
        for p in near:
            to = x_target(p)
            send(ob.at[slots_of(to), cols], zr.at[my_slots, cols], out_sem.at[6], cx_rs.at[kc], device(to, tp))

    def send_far(kc):
        part = pl.ds(kc * qw, qw)
        arrived(ob.at[pl.ds(0, others * 2 * cap), pl.ds(0, qw)], yf_rs.at[kc])
        for j, p in enumerate(far):
            to = x_target(p)
            total = ob[slots_of(to), quarter(kc, tp)]
            for i in range(others):
                total = total + yf[i, j, :, part]
            zs[j, :, part] = total
            send(zs.at[j, :, part], zr.at[my_slots, quarter(kc, tp)], out_sem.at[7], zf_rs.at[kc], device(to, tp))

    lead = CHUNKS // 2
    for kc in range(CHUNKS):
        down(kc)
        if kc < lead:
            send_near(kc)
    for kc in range(CHUNKS):
        send_far(kc)
        if kc + lead < CHUNKS:
            send_near(kc + lead)

    for kc in range(CHUNKS):
        cols = pl.ds(kc * kw, kw)
        arrived(zr.at[near_rows, cols], cx_rs.at[kc])
        arrived(zs.at[:, :, pl.ds(0, qw)], zf_rs.at[kc])
        z1, z2, z3 = split3(zr[:, cols])
        pick = row_of[...]
        yb[:, cols] = dot(pick, z3) + dot(pick, z2) + dot(pick, z1)
        for dt in (2, 1, 3):
            to = y_target(dt)
            send(yb.at[rows_at(to, rows), cols], yr.at[dt - 1, :, cols], out_sem.at[8], cy_rs.at[kc], device(ep, to))
    for kc in range(CHUNKS):
        cols = pl.ds(kc * kw, kw)
        arrived(yr.at[:, :, cols], cy_rs.at[kc])
        total = yb[my_rows, cols]
        for i in range(others):
            total = total + yr[i, :, cols]
        out_ref[:, cols] = total.astype(BF16)

    arrived(idg.at[pl.ds(0, others)], id_sem.at[0])
    arrived(gg.at[pl.ds(0, others)], id_sem.at[2])
    arrived(xg.at[pl.ds(0, others * rows)], out_sem.at[0])
    arrived(gr.at[pl.ds(0, len(x_peers))], out_sem.at[1])
    arrived(xs.at[pl.ds(0, 2 * cap), pl.ds(0, kw)], out_sem.at[2])
    arrived(xs.at[near_rows], out_sem.at[3])
    arrived(xs.at[pl.ds(0, others * 2 * cap), pl.ds(0, kw)], out_sem.at[4])
    arrived(yf, out_sem.at[5])
    arrived(ob.at[near_rows], out_sem.at[6])
    arrived(zs, out_sem.at[7])
    arrived(yr, out_sem.at[8])


def solution(mesh):
    ep_n = mesh.shape['ep']
    tp_n = mesh.shape['tp']
    names = tuple(mesh.axis_names)

    def block(tok, ids, gates, w_gate, w_up, w_down):
        rows, d = tok.shape
        local, _, hid = w_gate.shape
        choices = ids.shape[1]
        shard_rows = rows * tp_n
        slots = 2 * shard_rows
        cap = slots // ep_n
        ny = tp_n - 1
        any_spec = pl.BlockSpec(memory_space=pl.ANY)
        dma = pltpu.SemaphoreType.DMA
        return pl.pallas_call(
            functools.partial(moe_kernel, names, ep_n, tp_n),
            out_shape=pltpu.VMEM((rows, d), BF16),
            in_specs=[any_spec] * 6,
            out_specs=pl.BlockSpec(memory_space=pltpu.VMEM),
            scratch_shapes=[
                pltpu.VMEM((local, d, hid), BF16),
                pltpu.VMEM((local, d, hid), BF16),
                pltpu.VMEM((local, hid, d), BF16),
                pltpu.VMEM((shard_rows, d), BF16),
                pltpu.VMEM((tp_n, choices, rows), jnp.int32),
                pltpu.VMEM((tp_n, choices, rows), F32),
                pltpu.VMEM((slots, d), BF16),
                pltpu.VMEM((ep_n * local, slots), F32),
                pltpu.VMEM((slots, d), BF16),
                pltpu.VMEM((ep_n, local, LANES), F32),
                pltpu.VMEM((local, slots, hid), F32),
                pltpu.VMEM((local, slots, hid), F32),
                pltpu.VMEM((local, slots, hid), BF16),
                pltpu.VMEM((local, slots, LANES), F32),
                pltpu.VMEM((slots, d), F32),
                pltpu.VMEM((slots, d), F32),
                pltpu.VMEM((shard_rows, d), F32),
                pltpu.VMEM((ny, rows, d), F32),
                pltpu.VMEM((ny, 2, cap, d // tp_n), F32),
                pltpu.VMEM((2, cap, d // tp_n), F32),
                pltpu.VMEM((slots, shard_rows), BF16),
                pltpu.VMEM((shard_rows, slots), BF16),
                pltpu.VMEM((LANES, LANES), F32),
                dma((3,)), dma((3,)), dma((4,)), dma((CHUNKS,)), dma((1,)), dma((1,)), dma((CHUNKS,)), dma((ny,)),
                dma((CHUNKS,)), dma((CHUNKS,)), dma((CHUNKS,)), dma((CHUNKS,)), dma((9,)),
            ],
            compiler_params=pltpu.CompilerParams(collective_id=0, has_side_effects=True,
                                                 vmem_limit_bytes=60 * 1024 * 1024),
        )(tok, ids.T, gates.T, w_gate, w_up, w_down)

    return jax.shard_map(
        block,
        mesh=mesh,
        in_specs=(P(TOKEN_AXES, None), P(TOKEN_AXES, None), P(TOKEN_AXES, None),
                  P('ep', None, 'tp'), P('ep', None, 'tp'), P('ep', 'tp', None)),
        out_specs=P(TOKEN_AXES, None),
        check_vma=False,
    )
```

time: 58.3 us -> 52.1 us (0.89)
  Pallas kernels: 57.6 us -> 51.3 us
    pallas_call x1, Pallas kernels: 57.6 us -> 51.3 us  [block(): pl.pallas_call(functools.partial(moe_kernel, names, ep_n, tp_n), out_shap...]
where the time goes in v5:
time: 52.1 us; the launch traced here: 52 us
  Pallas kernels  51.3 us (98%)
  local copies, waits for them, and re-layouts  0.66 us (1%)
    pallas_call x1, Pallas kernels, block(): pl.pallas_call(functools.partial(moe_kernel, names, ep_n, tp_n), out_shap...  51.3 us

profile of v5, /device:TPU:97, one launch (start us, length us, event | category | flops | bytes accessed | tf_op | source)
XLA Modules:
  0.0 52.0 jit_solution(15357077187462325041)
XLA Ops:
  0.0 51.3 %shard_map.64 = bf16[32,2048]{1,0:T(8,128)(2,1)S(1)} custom-call(bf16[32,2048]{1,0:T(8,128)(2,1)} %tok_hbm.1, s32[8,32]{1,0:T(8,128)} %bitcast.2, f32[8,32]{1,0:T(8,128)} %bitcast.3, bf16[8,2048,256]{2,1,0:T(8,128)(2,1)} %wg_hbm.1, bf16[8,2048,256]{2,1,0:T(8,128)(2,1)} %wu_hbm.1, bf16[8,256,2048]{2,1,0:T(8,128)(2,1)} %wd_hbm.1), custom_call_target="tpu_custom_call" | custom-call | tf_op jit(solution)/shard_map/pallas_call | solution.py:296
  51.3 0.7 %copy.8 = bf16[32,2048]{1,0:T(8,128)(2,1)} copy(bf16[32,2048]{1,0:T(8,128)(2,1)S(1)} %shard_map.64) | data formatting | bytes 262144

commit v6 on v5

--- a/solution.py
+++ b/solution.py
@@ -81,6 +81,9 @@
     def chunk(t):
         return pl.ds(pl.multiple_of(t * kw, kw), kw)
 
+    def half(t, h):
+        return pl.ds(pl.multiple_of(t * kw + h * (kw // 2), kw // 2), kw // 2)
+
     def quarter(kc, t):
         return pl.ds(pl.multiple_of(kc * kw + t * qw, qw), qw)
 
@@ -111,10 +114,14 @@
         dev = device(ep, y_target(dt))
         send(idg.at[tp], idg.at[tp], id_sem.at[0], id_sem.at[1], dev)
         send(gg.at[tp], gg.at[tp], id_sem.at[2], id_sem.at[3], dev)
-    for kc in range(CHUNKS):
+    for h in range(2):
+        for dt in (2, 1, 3):
+            part = xg.at[my_rows, half(y_target(dt), h)]
+            send(part, part, out_sem.at[0], ag_rs.at[h], device(ep, y_target(dt)))
+    for kc in range(1, CHUNKS):
         for dt in (2, 1, 3):
             part = xg.at[my_rows, chunk(y_target(dt + turns[kc]))]
-            send(part, part, out_sem.at[0], ag_rs.at[kc], device(ep, y_target(dt)))
+            send(part, part, out_sem.at[0], ag_rs.at[kc + 1], device(ep, y_target(dt)))
     for i, (src, dst) in enumerate(((wg_hbm, wg), (wu_hbm, wu), (wd_hbm, wd))):
         for e in range(local):
             pltpu.make_async_copy(src.at[e], dst.at[e], w_sem.at[i]).start()
@@ -151,24 +158,29 @@
         send(gs.at[gate_tile(to)], gr.at[ep], out_sem.at[1], dg_rs.at[0], device(to, tp))
     gr[ep] = gs[gate_tile(ep)]
 
+    for h in range(2):
+        cols = half(tp, h)
+        arrived(xg.at[pl.ds(0, others * rows), pl.ds(0, kw // 2)], ag_rs.at[h])
+        xs[:, cols] = dot(slot_of[...], xg[:, cols]).astype(BF16)
+        for p in far:
+            to = x_target(p)
+            send(xs.at[slots_of(to), cols], xr.at[my_slots, cols], out_sem.at[2], df_rs.at[h], device(to, tp))
     for kc in range(CHUNKS):
         cols = chunk(y_target(turns[kc]))
-        arrived(xg.at[pl.ds(0, others * rows), pl.ds(0, kw)], ag_rs.at[kc])
-        xs[:, cols] = dot(slot_of[...], xg[:, cols]).astype(BF16)
-        if kc == 0:
-            for p in far:
-                to = x_target(p)
-                send(xs.at[slots_of(to), cols], xr.at[my_slots, cols], out_sem.at[2], df_rs.at[0], device(to, tp))
+        if kc > 0:
+            arrived(xg.at[pl.ds(0, others * rows), pl.ds(0, kw)], ag_rs.at[kc + 1])
+            xs[:, cols] = dot(slot_of[...], xg[:, cols]).astype(BF16)
         for p in near:
             to = x_target(p)
             send(xs.at[slots_of(to), cols], xr.at[my_slots, cols], out_sem.at[3], dx_rs.at[kc], device(to, tp))
         xr[my_slots, cols] = xs[my_slots, cols]
     row_of[...] = jnp.transpose(slot_of[...].astype(F32)).astype(BF16)
 
-    arrived(xs.at[pl.ds(0, 2 * cap), pl.ds(0, kw)], df_rs.at[0])
-    for dt in (3, 1, 2):
-        part = xr.at[far_slots, chunk(tp)]
-        send(part, part, out_sem.at[4], dq_rs.at[dt - 1], device(ep, y_target(dt)))
+    for h in range(2):
+        arrived(xs.at[pl.ds(0, 2 * cap), pl.ds(0, kw // 2)], df_rs.at[h])
+        for dt in (3, 1, 2):
+            part = xr.at[far_slots, half(tp, h)]
+            send(part, part, out_sem.at[4], dq_rs.at[dt - 1], device(ep, y_target(dt)))
 
     arrived(gr.at[pl.ds(0, len(x_peers))], dg_rs.at[0])
     lanes_of_mine = rows_at(lax.rem(ep, per_tile), cap)
@@ -242,10 +254,11 @@
         down(kc)
         if kc < lead:
             send_near(kc)
-    for kc in range(CHUNKS):
+    send_far(0)
+    for kc in range(1, CHUNKS):
         send_far(kc)
-        if kc + lead < CHUNKS:
-            send_near(kc + lead)
+        if kc + lead <= CHUNKS:
+            send_near(kc + lead - 1)
 
     for kc in range(CHUNKS):
         cols = pl.ds(kc * kw, kw)
@@ -322,7 +335,7 @@
                 pltpu.VMEM((slots, shard_rows), BF16),
                 pltpu.VMEM((shard_rows, slots), BF16),
                 pltpu.VMEM((LANES, LANES), F32),
-                dma((3,)), dma((3,)), dma((4,)), dma((CHUNKS,)), dma((1,)), dma((1,)), dma((CHUNKS,)), dma((ny,)),
+                dma((3,)), dma((3,)), dma((4,)), dma((CHUNKS + 1,)), dma((1,)), dma((2,)), dma((CHUNKS,)), dma((ny,)),
                 dma((CHUNKS,)), dma((CHUNKS,)), dma((CHUNKS,)), dma((CHUNKS,)), dma((9,)),
             ],
             compiler_params=pltpu.CompilerParams(collective_id=0, has_side_effects=True,

time: 52.1 us -> 49.4 us (0.948)
  Pallas kernels: 51.3 us -> 48.7 us
    pallas_call x1, Pallas kernels: 51.3 us -> 48.7 us  [block(): pl.pallas_call(functools.partial(moe_kernel, names, ep_n, tp_n), out_shap...]
where the time goes in v6:
time: 49.4 us; the launch traced here: 49.3 us
  Pallas kernels  48.7 us (99%)
  local copies, waits for them, and re-layouts  0.66 us (1%)
    pallas_call x1, Pallas kernels, block(): pl.pallas_call(functools.partial(moe_kernel, names, ep_n, tp_n), out_shap...  48.7 us

profile of v6, /device:TPU:97, one launch (start us, length us, event | category | flops | bytes accessed | tf_op | source)
XLA Modules:
  0.0 49.3 jit_solution(3390644861153333017)
XLA Ops:
  0.0 48.7 %shard_map.64 = bf16[32,2048]{1,0:T(8,128)(2,1)S(1)} custom-call(bf16[32,2048]{1,0:T(8,128)(2,1)} %tok_hbm.1, s32[8,32]{1,0:T(8,128)} %bitcast.2, f32[8,32]{1,0:T(8,128)} %bitcast.3, bf16[8,2048,256]{2,1,0:T(8,128)(2,1)} %wg_hbm.1, bf16[8,2048,256]{2,1,0:T(8,128)(2,1)} %wu_hbm.1, bf16[8,256,2048]{2,1,0:T(8,128)(2,1)} %wd_hbm.1), custom_call_target="tpu_custom_call" | custom-call | tf_op jit(solution)/shard_map/pallas_call | solution.py:309
  48.7 0.7 %copy.8 = bf16[32,2048]{1,0:T(8,128)(2,1)} copy(bf16[32,2048]{1,0:T(8,128)(2,1)S(1)} %shard_map.64) | data formatting | bytes 262144

commit v7 on v6

--- a/solution.py
+++ b/solution.py
@@ -10,6 +10,7 @@
 TOKEN_AXES = ('dp', 'ep', 'tp')
 LANES = 128
 CHUNKS = 4
+STRAIGHT = 2
 F32 = jnp.float32
 BF16 = jnp.bfloat16
 MESH = pl.DeviceIdType.MESH
@@ -36,9 +37,9 @@
 
 
 def moe_kernel(names, ep_n, tp_n, tok_hbm, ids_hbm, gate_hbm, wg_hbm, wu_hbm, wd_hbm, out_ref,
-               wg, wu, wd, xg, idg, gg, xs, gs, xr, gr, acc_g, acc_u, hb, gb, ob, zr, yb, yr, yf, zs,
+               wg, wu, wd, xg, idg, gg, xs, gs, xr, gr, acc_g, acc_u, hb, gb, ob, zr, yb, yr, pr, zs,
                slot_of, row_of, gcols,
-               w_sem, in_sem, id_sem, ag_rs, dg_rs, df_rs, dx_rs, dq_rs, cx_rs, yf_rs, zf_rs, cy_rs, out_sem):
+               w_sem, in_sem, id_sem, ag_rs, dg_rs, df_rs, dx_rs, dq_rs, pr_rs, cx_rs, cy_rs, out_sem):
     rows, d = tok_hbm.shape
     local = wg_hbm.shape[0]
     choices = ids_hbm.shape[0]
@@ -47,7 +48,8 @@
     slots = cap * ep_n
     per_tile = LANES // cap
     kw = d // CHUNKS
-    qw = kw // tp_n
+    unit = 2 * LANES
+    units = d // unit
     chips = ep_n // 2
 
     ep = lax.axis_index('ep')
@@ -83,9 +85,6 @@
 
     def half(t, h):
         return pl.ds(pl.multiple_of(t * kw + h * (kw // 2), kw // 2), kw // 2)
-
-    def quarter(kc, t):
-        return pl.ds(pl.multiple_of(kc * kw + t * qw, qw), qw)
 
     my_rows = rows_at(tp, rows)
     my_slots = slots_of(ep)
@@ -98,8 +97,6 @@
            pltpu.make_async_copy(tok_hbm, xg.at[my_rows], in_sem.at[2])]
     for c in own:
         c.start()
-
-    zr[far_slots, :] = jnp.zeros((2 * cap, d), F32)
 
     bar = pltpu.get_barrier_semaphore()
     for dt in range(1, tp_n):
@@ -217,66 +214,75 @@
         lax.fori_loop(0, local, up, 0, unroll=True)
 
     arrived(wd, w_sem.at[2])
-
-    def down(kc):
-        cols = pl.ds(kc * kw, kw)
+    parity = lax.rem(tp, 2)
+    pairs = (tp + 1 - 2 * parity, y_target(tp_n - 1 + 2 * parity))
+    group = slots // 2
+
+    def span(u):
+        return pl.ds(u * unit, unit)
+
+    def mine(u):
+        return pl.ds(pl.multiple_of(u * unit + parity * LANES, LANES), LANES)
+
+    def theirs(u):
+        return pl.ds(pl.multiple_of(u * unit + (1 - parity) * LANES, LANES), LANES)
+
+    def packed(u):
+        return pl.ds((u - STRAIGHT) * LANES, LANES)
+
+    def down(u):
+        cols = span(u)
         total = None
         for e in range(local):
-            o = dot(hb[e], wd[e, :, cols]) * jnp.concatenate([gb[e]] * (kw // LANES), axis=1)
+            o = dot(hb[e], wd[e, :, cols]) * jnp.concatenate([gb[e]] * (unit // LANES), axis=1)
             total = o if total is None else total + o
         ob[:, cols] = total
-        zr[my_slots, cols] = ob[my_slots, cols]
-        for j, p in enumerate(far):
-            for dt in (2, 1, 3):
-                q = y_target(dt)
-                send(ob.at[slots_of(x_target(p)), quarter(kc, q)], yf.at[dt - 1, j, :, pl.ds(kc * qw, qw)],
-                     out_sem.at[5], yf_rs.at[kc], device(ep, q))
-
-    def send_near(kc):
-        cols = pl.ds(kc * kw, kw)
-        for p in near:
+        if u < STRAIGHT:
+            for p in x_peers:
+                to = x_target(p)
+                send(ob.at[slots_of(to), cols], zr.at[my_slots, cols], out_sem.at[5], cx_rs.at[u], device(to, tp))
+            zr[my_slots, cols] = ob[my_slots, cols]
+        else:
+            for g, to in enumerate(pairs):
+                part = pl.ds(g * group, group)
+                send(ob.at[part, theirs(u)], pr.at[part, packed(u)], out_sem.at[6], pr_rs.at[u], device(ep, to))
+
+    def pair_sum(u):
+        arrived(pr.at[:, packed(u)], pr_rs.at[u])
+        zs[:, packed(u)] = ob[:, mine(u)] + pr[:, packed(u)]
+        for p in x_peers:
             to = x_target(p)
-            send(ob.at[slots_of(to), cols], zr.at[my_slots, cols], out_sem.at[6], cx_rs.at[kc], device(to, tp))
-
-    def send_far(kc):
-        part = pl.ds(kc * qw, qw)
-        arrived(ob.at[pl.ds(0, others * 2 * cap), pl.ds(0, qw)], yf_rs.at[kc])
-        for j, p in enumerate(far):
-            to = x_target(p)
-            total = ob[slots_of(to), quarter(kc, tp)]
-            for i in range(others):
-                total = total + yf[i, j, :, part]
-            zs[j, :, part] = total
-            send(zs.at[j, :, part], zr.at[my_slots, quarter(kc, tp)], out_sem.at[7], zf_rs.at[kc], device(to, tp))
-
-    lead = CHUNKS // 2
-    for kc in range(CHUNKS):
-        down(kc)
-        if kc < lead:
-            send_near(kc)
-    send_far(0)
-    for kc in range(1, CHUNKS):
-        send_far(kc)
-        if kc + lead <= CHUNKS:
-            send_near(kc + lead - 1)
-
-    for kc in range(CHUNKS):
-        cols = pl.ds(kc * kw, kw)
-        arrived(zr.at[near_rows, cols], cx_rs.at[kc])
-        arrived(zs.at[:, :, pl.ds(0, qw)], zf_rs.at[kc])
+            send(zs.at[slots_of(to), packed(u)], zr.at[my_slots, mine(u)], out_sem.at[5], cx_rs.at[u], device(to, tp))
+        zr[my_slots, mine(u)] = zs[my_slots, packed(u)]
+
+    def combine(u):
+        cols, width = (span(u), unit) if u < STRAIGHT else (mine(u), LANES)
+        arrived(zr.at[pl.ds(0, len(x_peers) * cap), pl.ds(0, width)], cx_rs.at[u])
         z1, z2, z3 = split3(zr[:, cols])
         pick = row_of[...]
         yb[:, cols] = dot(pick, z3) + dot(pick, z2) + dot(pick, z1)
         for dt in (2, 1, 3):
             to = y_target(dt)
-            send(yb.at[rows_at(to, rows), cols], yr.at[dt - 1, :, cols], out_sem.at[8], cy_rs.at[kc], device(ep, to))
-    for kc in range(CHUNKS):
-        cols = pl.ds(kc * kw, kw)
-        arrived(yr.at[:, :, cols], cy_rs.at[kc])
-        total = yb[my_rows, cols]
-        for i in range(others):
-            total = total + yr[i, :, cols]
-        out_ref[:, cols] = total.astype(BF16)
+            send(yb.at[rows_at(to, rows), cols], yr.at[dt - 1, :, cols], out_sem.at[7], cy_rs.at[u], device(ep, to))
+
+    def finish(u):
+        width = unit if u < STRAIGHT else LANES
+        arrived(yr.at[:, :, pl.ds(0, width)], cy_rs.at[u])
+        if u < STRAIGHT:
+            cols = span(u)
+            out_ref[:, cols] = (yb[my_rows, cols] + yr[0, :, cols] + yr[1, :, cols] + yr[2, :, cols]).astype(BF16)
+        else:
+            out_ref[:, mine(u)] = (yb[my_rows, mine(u)] + yr[1, :, mine(u)]).astype(BF16)
+            out_ref[:, theirs(u)] = (yr[0, :, theirs(u)] + yr[2, :, theirs(u)]).astype(BF16)
+
+    for u in (0, 2, 3, 1, 4, 5, 6, 7):
+        down(u)
+    for step, u in ((pair_sum, 2), (combine, 0), (pair_sum, 3), (pair_sum, 4), (combine, 1), (pair_sum, 5),
+                    (combine, 2), (pair_sum, 6), (combine, 3), (pair_sum, 7), (combine, 4), (combine, 5),
+                    (combine, 6), (combine, 7)):
+        step(u)
+    for u in range(units):
+        finish(u)
 
     arrived(idg.at[pl.ds(0, others)], id_sem.at[0])
     arrived(gg.at[pl.ds(0, others)], id_sem.at[2])
@@ -285,10 +291,11 @@
     arrived(xs.at[pl.ds(0, 2 * cap), pl.ds(0, kw)], out_sem.at[2])
     arrived(xs.at[near_rows], out_sem.at[3])
     arrived(xs.at[pl.ds(0, others * 2 * cap), pl.ds(0, kw)], out_sem.at[4])
-    arrived(yf, out_sem.at[5])
-    arrived(ob.at[near_rows], out_sem.at[6])
-    arrived(zs, out_sem.at[7])
-    arrived(yr, out_sem.at[8])
+    paired = units - STRAIGHT
+    sent = pl.ds(0, STRAIGHT * unit + paired * LANES)
+    arrived(ob.at[pl.ds(0, len(x_peers) * cap), sent], out_sem.at[5])
+    arrived(pr, out_sem.at[6])
+    arrived(yr.at[:, :, sent], out_sem.at[7])
 
 
 def solution(mesh):
@@ -304,6 +311,7 @@
         slots = 2 * shard_rows
         cap = slots // ep_n
         ny = tp_n - 1
+        units = d // (2 * LANES)
         any_spec = pl.BlockSpec(memory_space=pl.ANY)
         dma = pltpu.SemaphoreType.DMA
         return pl.pallas_call(
@@ -330,13 +338,13 @@
                 pltpu.VMEM((slots, d), F32),
                 pltpu.VMEM((shard_rows, d), F32),
                 pltpu.VMEM((ny, rows, d), F32),
-                pltpu.VMEM((ny, 2, cap, d // tp_n), F32),
-                pltpu.VMEM((2, cap, d // tp_n), F32),
+                pltpu.VMEM((slots, d // 2 - STRAIGHT * LANES), F32),
+                pltpu.VMEM((slots, d // 2 - STRAIGHT * LANES), F32),
                 pltpu.VMEM((slots, shard_rows), BF16),
                 pltpu.VMEM((shard_rows, slots), BF16),
                 pltpu.VMEM((LANES, LANES), F32),
                 dma((3,)), dma((3,)), dma((4,)), dma((CHUNKS + 1,)), dma((1,)), dma((2,)), dma((CHUNKS,)), dma((ny,)),
-                dma((CHUNKS,)), dma((CHUNKS,)), dma((CHUNKS,)), dma((CHUNKS,)), dma((9,)),
+                dma((units,)), dma((units,)), dma((units,)), dma((8,)),
             ],
             compiler_params=pltpu.CompilerParams(collective_id=0, has_side_effects=True,
                                                  vmem_limit_bytes=60 * 1024 * 1024),

time: 49.4 us -> 45.6 us (0.923)
  Pallas kernels: 48.7 us -> 44.8 us
    pallas_call x1, Pallas kernels: 48.7 us -> 44.8 us  [block(): pl.pallas_call(functools.partial(moe_kernel, names, ep_n, tp_n), out_shap...]
where the time goes in v7:
time: 45.6 us; the launch traced here: 45.5 us
  Pallas kernels  44.8 us (98%)
  local copies, waits for them, and re-layouts  0.66 us (1%)
    pallas_call x1, Pallas kernels, block(): pl.pallas_call(functools.partial(moe_kernel, names, ep_n, tp_n), out_shap...  44.8 us

profile of v7, /device:TPU:97, one launch (start us, length us, event | category | flops | bytes accessed | tf_op | source)
XLA Modules:
  0.0 45.5 jit_solution(4039216935215193412)
XLA Ops:
  0.0 44.8 %shard_map.64 = bf16[32,2048]{1,0:T(8,128)(2,1)S(1)} custom-call(bf16[32,2048]{1,0:T(8,128)(2,1)} %tok_hbm.1, s32[8,32]{1,0:T(8,128)} %bitcast.2, f32[8,32]{1,0:T(8,128)} %bitcast.3, bf16[8,2048,256]{2,1,0:T(8,128)(2,1)} %wg_hbm.1, bf16[8,2048,256]{2,1,0:T(8,128)(2,1)} %wu_hbm.1, bf16[8,256,2048]{2,1,0:T(8,128)(2,1)} %wd_hbm.1), custom_call_target="tpu_custom_call" | custom-call | tf_op jit(solution)/shard_map/pallas_call | solution.py:317
  44.8 0.7 %copy.8 = bf16[32,2048]{1,0:T(8,128)(2,1)} copy(bf16[32,2048]{1,0:T(8,128)(2,1)S(1)} %shard_map.64) | data formatting | bytes 262144

commit v8 on v7

--- a/solution.py
+++ b/solution.py
@@ -162,7 +162,7 @@
         for p in far:
             to = x_target(p)
             send(xs.at[slots_of(to), cols], xr.at[my_slots, cols], out_sem.at[2], df_rs.at[h], device(to, tp))
-    for kc in range(CHUNKS):
+    def pack(kc):
         cols = chunk(y_target(turns[kc]))
         if kc > 0:
             arrived(xg.at[pl.ds(0, others * rows), pl.ds(0, kw)], ag_rs.at[kc + 1])
@@ -171,13 +171,20 @@
             to = x_target(p)
             send(xs.at[slots_of(to), cols], xr.at[my_slots, cols], out_sem.at[3], dx_rs.at[kc], device(to, tp))
         xr[my_slots, cols] = xs[my_slots, cols]
-    row_of[...] = jnp.transpose(slot_of[...].astype(F32)).astype(BF16)
-
+
+    def spread(cols, dts):
+        for dt in dts:
+            part = xr.at[far_slots, cols]
+            send(part, part, out_sem.at[4], dq_rs.at[dt - 1], device(ep, y_target(dt)))
+
+    for kc in range(CHUNKS - 1):
+        pack(kc)
     for h in range(2):
         arrived(xs.at[pl.ds(0, 2 * cap), pl.ds(0, kw // 2)], df_rs.at[h])
-        for dt in (3, 1, 2):
-            part = xr.at[far_slots, half(tp, h)]
-            send(part, part, out_sem.at[4], dq_rs.at[dt - 1], device(ep, y_target(dt)))
+        spread(half(tp, h), (3, 1))
+    spread(chunk(tp), (2,))
+    pack(CHUNKS - 1)
+    row_of[...] = jnp.transpose(slot_of[...].astype(F32)).astype(BF16)
 
     arrived(gr.at[pl.ds(0, len(x_peers))], dg_rs.at[0])
     lanes_of_mine = rows_at(lax.rem(ep, per_tile), cap)
@@ -189,20 +196,25 @@
 
     arrived(wg, w_sem.at[0])
     arrived(wu, w_sem.at[1])
-    for kc in range(CHUNKS):
-        cols = chunk(y_target(turns[kc]))
-        arrived(xr.at[near_rows, pl.ds(0, kw)], dx_rs.at[kc])
-        if kc > 0:
-            arrived(xr.at[pl.ds(0, 2 * cap), pl.ds(0, kw)], dq_rs.at[tp_n - turns[kc] - 1])
-
-        def up(e, carry, kc=kc, cols=cols):
-            x = xr[:, cols]
-            a = dot(x, wg[e, cols, :])
-            b = dot(x, wu[e, cols, :])
+    for kcs in ((0,), (1,), (2, 3)):
+        for kc in kcs:
+            arrived(xr.at[near_rows, pl.ds(0, kw)], dx_rs.at[kc])
             if kc > 0:
+                arrived(xr.at[pl.ds(0, 2 * cap), pl.ds(0, kw)], dq_rs.at[tp_n - turns[kc] - 1])
+
+        def up(e, carry, kcs=kcs):
+            a = b = None
+            for kc in kcs:
+                cols = chunk(y_target(turns[kc]))
+                x = xr[:, cols]
+                a_k = dot(x, wg[e, cols, :])
+                b_k = dot(x, wu[e, cols, :])
+                a = a_k if a is None else a + a_k
+                b = b_k if b is None else b + b_k
+            if kcs[0] > 0:
                 a = a + acc_g[e]
                 b = b + acc_u[e]
-            if kc < CHUNKS - 1:
+            if kcs[-1] < CHUNKS - 1:
                 acc_g[e] = a
                 acc_u[e] = b
             else:

time: 45.6 us -> 46.1 us (1.011)
  Pallas kernels: 44.8 us -> 45.4 us
    pallas_call x1, Pallas kernels: 44.8 us -> 45.4 us  [block(): pl.pallas_call(functools.partial(moe_kernel, names, ep_n, tp_n), out_shap...]
where the time goes in v8:
time: 46.1 us
  Pallas kernels  45.4 us (98%)
  local copies, waits for them, and re-layouts  0.66 us (1%)
    pallas_call x1, Pallas kernels, block(): pl.pallas_call(functools.partial(moe_kernel, names, ep_n, tp_n), out_shap...  45.4 us

profile of v8, /device:TPU:97, one launch (start us, length us, event | category | flops | bytes accessed | tf_op | source)
XLA Modules:
  0.0 46.1 jit_solution(9220260877663591041)
XLA Ops:
  0.0 45.4 %shard_map.64 = bf16[32,2048]{1,0:T(8,128)(2,1)S(1)} custom-call(bf16[32,2048]{1,0:T(8,128)(2,1)} %tok_hbm.1, s32[8,32]{1,0:T(8,128)} %bitcast.2, f32[8,32]{1,0:T(8,128)} %bitcast.3, bf16[8,2048,256]{2,1,0:T(8,128)(2,1)} %wg_hbm.1, bf16[8,2048,256]{2,1,0:T(8,128)(2,1)} %wu_hbm.1, bf16[8,256,2048]{2,1,0:T(8,128)(2,1)} %wd_hbm.1), custom_call_target="tpu_custom_call" | custom-call | tf_op jit(solution)/shard_map/pallas_call | solution.py:329
  45.4 0.7 %copy.8 = bf16[32,2048]{1,0:T(8,128)(2,1)} copy(bf16[32,2048]{1,0:T(8,128)(2,1)S(1)} %shard_map.64) | data formatting | bytes 262144

commit v9 on v8

--- a/solution.py
+++ b/solution.py
@@ -177,13 +177,12 @@
             part = xr.at[far_slots, cols]
             send(part, part, out_sem.at[4], dq_rs.at[dt - 1], device(ep, y_target(dt)))
 
-    for kc in range(CHUNKS - 1):
+    for kc in range(CHUNKS):
         pack(kc)
     for h in range(2):
         arrived(xs.at[pl.ds(0, 2 * cap), pl.ds(0, kw // 2)], df_rs.at[h])
         spread(half(tp, h), (3, 1))
     spread(chunk(tp), (2,))
-    pack(CHUNKS - 1)
     row_of[...] = jnp.transpose(slot_of[...].astype(F32)).astype(BF16)
 
     arrived(gr.at[pl.ds(0, len(x_peers))], dg_rs.at[0])

time: 46.1 us -> 45.7 us (level)
  Pallas kernels: 45.4 us -> 44.9 us
where the time goes in v9:
time: 45.7 us; the launch traced here: 45.6 us
  Pallas kernels  44.9 us (98%)
  local copies, waits for them, and re-layouts  0.66 us (1%)
    pallas_call x1, Pallas kernels, block(): pl.pallas_call(functools.partial(moe_kernel, names, ep_n, tp_n), out_shap...  44.9 us

profile of v9, /device:TPU:97, one launch (start us, length us, event | category | flops | bytes accessed | tf_op | source)
XLA Modules:
  0.0 45.6 jit_solution(13409450758624949363)
XLA Ops:
  0.0 44.9 %shard_map.64 = bf16[32,2048]{1,0:T(8,128)(2,1)S(1)} custom-call(bf16[32,2048]{1,0:T(8,128)(2,1)} %tok_hbm.1, s32[8,32]{1,0:T(8,128)} %bitcast.2, f32[8,32]{1,0:T(8,128)} %bitcast.3, bf16[8,2048,256]{2,1,0:T(8,128)(2,1)} %wg_hbm.1, bf16[8,2048,256]{2,1,0:T(8,128)(2,1)} %wu_hbm.1, bf16[8,256,2048]{2,1,0:T(8,128)(2,1)} %wd_hbm.1), custom_call_target="tpu_custom_call" | custom-call | tf_op jit(solution)/shard_map/pallas_call | solution.py:328
  44.9 0.7 %copy.8 = bf16[32,2048]{1,0:T(8,128)(2,1)} copy(bf16[32,2048]{1,0:T(8,128)(2,1)S(1)} %shard_map.64) | data formatting | bytes 262144

commit v10 on v9

--- a/solution.py
+++ b/solution.py
@@ -62,13 +62,19 @@
     far = [(chips // 2, 0), (chips // 2, 1)]
     near = [(1, 0), (1, 1), (chips - 1, 0), (chips - 1, 1), (0, 1)]
     x_peers = far + near
-    turns = (0, 1, tp_n - 1, 2)
+    parity = lax.rem(tp, 2)
+    sign = 1 - 2 * parity
+
+    def turn(k, s):
+        return (0, s, -s, 2)[k]
+
+    peers = ((sign, -sign), (-sign, -sign), (2, sign))
 
     def x_target(p):
         return lax.rem(ep // 2 + p[0], chips) * 2 + lax.rem(ep + p[1], 2)
 
     def y_target(dt):
-        return lax.rem(tp + dt, tp_n)
+        return lax.rem(tp + dt + tp_n, tp_n)
 
     def send(src, dst, ss, rs, dev):
         pltpu.make_async_remote_copy(src_ref=src, dst_ref=dst, send_sem=ss, recv_sem=rs,
@@ -112,12 +118,12 @@
         send(idg.at[tp], idg.at[tp], id_sem.at[0], id_sem.at[1], dev)
         send(gg.at[tp], gg.at[tp], id_sem.at[2], id_sem.at[3], dev)
     for h in range(2):
-        for dt in (2, 1, 3):
+        for dt, _ in peers:
             part = xg.at[my_rows, half(y_target(dt), h)]
             send(part, part, out_sem.at[0], ag_rs.at[h], device(ep, y_target(dt)))
     for kc in range(1, CHUNKS):
-        for dt in (2, 1, 3):
-            part = xg.at[my_rows, chunk(y_target(dt + turns[kc]))]
+        for dt, s in peers:
+            part = xg.at[my_rows, chunk(y_target(dt + turn(kc, s)))]
             send(part, part, out_sem.at[0], ag_rs.at[kc + 1], device(ep, y_target(dt)))
     for i, (src, dst) in enumerate(((wg_hbm, wg), (wu_hbm, wu), (wd_hbm, wd))):
         for e in range(local):
@@ -163,7 +169,7 @@
             to = x_target(p)
             send(xs.at[slots_of(to), cols], xr.at[my_slots, cols], out_sem.at[2], df_rs.at[h], device(to, tp))
     def pack(kc):
-        cols = chunk(y_target(turns[kc]))
+        cols = chunk(y_target(turn(kc, sign)))
         if kc > 0:
             arrived(xg.at[pl.ds(0, others * rows), pl.ds(0, kw)], ag_rs.at[kc + 1])
             xs[:, cols] = dot(slot_of[...], xg[:, cols]).astype(BF16)
@@ -172,17 +178,17 @@
             send(xs.at[slots_of(to), cols], xr.at[my_slots, cols], out_sem.at[3], dx_rs.at[kc], device(to, tp))
         xr[my_slots, cols] = xs[my_slots, cols]
 
-    def spread(cols, dts):
-        for dt in dts:
+    def spread(cols, ks):
+        for k in ks:
             part = xr.at[far_slots, cols]
-            send(part, part, out_sem.at[4], dq_rs.at[dt - 1], device(ep, y_target(dt)))
+            send(part, part, out_sem.at[4], dq_rs.at[k - 1], device(ep, y_target(turn(k, sign))))
 
     for kc in range(CHUNKS):
         pack(kc)
     for h in range(2):
         arrived(xs.at[pl.ds(0, 2 * cap), pl.ds(0, kw // 2)], df_rs.at[h])
-        spread(half(tp, h), (3, 1))
-    spread(chunk(tp), (2,))
+        spread(half(tp, h), (1, 2))
+    spread(chunk(tp), (3,))
     row_of[...] = jnp.transpose(slot_of[...].astype(F32)).astype(BF16)
 
     arrived(gr.at[pl.ds(0, len(x_peers))], dg_rs.at[0])
@@ -199,12 +205,12 @@
         for kc in kcs:
             arrived(xr.at[near_rows, pl.ds(0, kw)], dx_rs.at[kc])
             if kc > 0:
-                arrived(xr.at[pl.ds(0, 2 * cap), pl.ds(0, kw)], dq_rs.at[tp_n - turns[kc] - 1])
+                arrived(xr.at[pl.ds(0, 2 * cap), pl.ds(0, kw)], dq_rs.at[kc - 1])
 
         def up(e, carry, kcs=kcs):
             a = b = None
             for kc in kcs:
-                cols = chunk(y_target(turns[kc]))
+                cols = chunk(y_target(turn(kc, sign)))
                 x = xr[:, cols]
                 a_k = dot(x, wg[e, cols, :])
                 b_k = dot(x, wu[e, cols, :])
@@ -225,7 +231,6 @@
         lax.fori_loop(0, local, up, 0, unroll=True)
 
     arrived(wd, w_sem.at[2])
-    parity = lax.rem(tp, 2)
     pairs = (tp + 1 - 2 * parity, y_target(tp_n - 1 + 2 * parity))
     group = slots // 2
 

time: 45.7 us -> 45.6 us (level)
  no operation moved by 1% of the time
where the time goes in v10:
time: 45.6 us; the launch traced here: 45.5 us
  Pallas kernels  44.9 us (98%)
  local copies, waits for them, and re-layouts  0.66 us (1%)
    pallas_call x1, Pallas kernels, block(): pl.pallas_call(functools.partial(moe_kernel, names, ep_n, tp_n), out_shap...  44.9 us

profile of v10, /device:TPU:97, one launch (start us, length us, event | category | flops | bytes accessed | tf_op | source)
XLA Modules:
  0.0 45.5 jit_solution(6038327825141405726)
XLA Ops:
  0.0 44.9 %shard_map.64 = bf16[32,2048]{1,0:T(8,128)(2,1)S(1)} custom-call(bf16[32,2048]{1,0:T(8,128)(2,1)} %tok_hbm.1, s32[8,32]{1,0:T(8,128)} %bitcast.2, f32[8,32]{1,0:T(8,128)} %bitcast.3, bf16[8,2048,256]{2,1,0:T(8,128)(2,1)} %wg_hbm.1, bf16[8,2048,256]{2,1,0:T(8,128)(2,1)} %wu_hbm.1, bf16[8,256,2048]{2,1,0:T(8,128)(2,1)} %wd_hbm.1), custom_call_target="tpu_custom_call" | custom-call | tf_op jit(solution)/shard_map/pallas_call | solution.py:333
  44.9 0.7 %copy.8 = bf16[32,2048]{1,0:T(8,128)(2,1)} copy(bf16[32,2048]{1,0:T(8,128)(2,1)S(1)} %shard_map.64) | data formatting | bytes 262144

commit v11 on v10

--- a/solution.py
+++ b/solution.py
@@ -201,7 +201,7 @@
 
     arrived(wg, w_sem.at[0])
     arrived(wu, w_sem.at[1])
-    for kcs in ((0,), (1,), (2, 3)):
+    for kcs in ((0,), (1,), (2,), (3,)):
         for kc in kcs:
             arrived(xr.at[near_rows, pl.ds(0, kw)], dx_rs.at[kc])
             if kc > 0:

time: 45.6 us -> 44.7 us (0.980)
  Pallas kernels: 44.9 us -> 44 us
    pallas_call x1, Pallas kernels: 44.9 us -> 44 us  [block(): pl.pallas_call(functools.partial(moe_kernel, names, ep_n, tp_n), out_shap...]
where the time goes in v11:
time: 44.7 us; the launch traced here: 44.6 us
  Pallas kernels  44 us (98%)
  local copies, waits for them, and re-layouts  0.66 us (1%)
    pallas_call x1, Pallas kernels, block(): pl.pallas_call(functools.partial(moe_kernel, names, ep_n, tp_n), out_shap...  44 us

profile of v11, /device:TPU:97, one launch (start us, length us, event | category | flops | bytes accessed | tf_op | source)
XLA Modules:
  0.0 44.6 jit_solution(5770631668036651846)
XLA Ops:
  0.0 44.0 %shard_map.64 = bf16[32,2048]{1,0:T(8,128)(2,1)S(1)} custom-call(bf16[32,2048]{1,0:T(8,128)(2,1)} %tok_hbm.1, s32[8,32]{1,0:T(8,128)} %bitcast.2, f32[8,32]{1,0:T(8,128)} %bitcast.3, bf16[8,2048,256]{2,1,0:T(8,128)(2,1)} %wg_hbm.1, bf16[8,2048,256]{2,1,0:T(8,128)(2,1)} %wu_hbm.1, bf16[8,256,2048]{2,1,0:T(8,128)(2,1)} %wd_hbm.1), custom_call_target="tpu_custom_call" | custom-call | tf_op jit(solution)/shard_map/pallas_call | solution.py:333
  44.0 0.7 %copy.8 = bf16[32,2048]{1,0:T(8,128)(2,1)} copy(bf16[32,2048]{1,0:T(8,128)(2,1)S(1)} %shard_map.64) | data formatting | bytes 262144

commit v12 on v11

--- a/solution.py
+++ b/solution.py
@@ -68,7 +68,7 @@
     def turn(k, s):
         return (0, s, -s, 2)[k]
 
-    peers = ((sign, -sign), (-sign, -sign), (2, sign))
+    peers = ((2, sign), (sign, -sign), (-sign, -sign))
 
     def x_target(p):
         return lax.rem(ep // 2 + p[0], chips) * 2 + lax.rem(ep + p[1], 2)
@@ -293,8 +293,8 @@
 
     for u in (0, 2, 3, 1, 4, 5, 6, 7):
         down(u)
-    for step, u in ((pair_sum, 2), (combine, 0), (pair_sum, 3), (pair_sum, 4), (combine, 1), (pair_sum, 5),
-                    (combine, 2), (pair_sum, 6), (combine, 3), (pair_sum, 7), (combine, 4), (combine, 5),
+    for step, u in ((pair_sum, 2), (pair_sum, 3), (combine, 0), (pair_sum, 4), (pair_sum, 5), (combine, 1),
+                    (pair_sum, 6), (combine, 2), (pair_sum, 7), (combine, 3), (combine, 4), (combine, 5),
                     (combine, 6), (combine, 7)):
         step(u)
     for u in range(units):

time: 44.7 us -> 44.4 us (level)
  no operation moved by 1% of the time
where the time goes in v12:
time: 44.4 us; the launch traced here: 44.3 us
  Pallas kernels  43.6 us (98%)
  local copies, waits for them, and re-layouts  0.66 us (1%)
    pallas_call x1, Pallas kernels, block(): pl.pallas_call(functools.partial(moe_kernel, names, ep_n, tp_n), out_shap...  43.6 us

profile of v12, /device:TPU:97, one launch (start us, length us, event | category | flops | bytes accessed | tf_op | source)
XLA Modules:
  0.0 44.3 jit_solution(4659717439200678776)
XLA Ops:
  0.0 43.6 %shard_map.64 = bf16[32,2048]{1,0:T(8,128)(2,1)S(1)} custom-call(bf16[32,2048]{1,0:T(8,128)(2,1)} %tok_hbm.1, s32[8,32]{1,0:T(8,128)} %bitcast.2, f32[8,32]{1,0:T(8,128)} %bitcast.3, bf16[8,2048,256]{2,1,0:T(8,128)(2,1)} %wg_hbm.1, bf16[8,2048,256]{2,1,0:T(8,128)(2,1)} %wu_hbm.1, bf16[8,256,2048]{2,1,0:T(8,128)(2,1)} %wd_hbm.1), custom_call_target="tpu_custom_call" | custom-call | tf_op jit(solution)/shard_map/pallas_call | solution.py:333
  43.6 0.7 %copy.8 = bf16[32,2048]{1,0:T(8,128)(2,1)} copy(bf16[32,2048]{1,0:T(8,128)(2,1)S(1)} %shard_map.64) | data formatting | bytes 262144

commit v13 on v12

--- a/solution.py
+++ b/solution.py
@@ -39,7 +39,7 @@
 def moe_kernel(names, ep_n, tp_n, tok_hbm, ids_hbm, gate_hbm, wg_hbm, wu_hbm, wd_hbm, out_ref,
                wg, wu, wd, xg, idg, gg, xs, gs, xr, gr, acc_g, acc_u, hb, gb, ob, zr, yb, yr, pr, zs,
                slot_of, row_of, gcols,
-               w_sem, in_sem, id_sem, ag_rs, dg_rs, df_rs, dx_rs, dq_rs, pr_rs, cx_rs, cy_rs, out_sem):
+               w_sem, in_sem, id_sem, ag_rs, dg_rs, df_rs, dx_rs, dq_rs, pr_rs, cx_rs, cf_rs, cy_rs, out_sem):
     rows, d = tok_hbm.shape
     local = wg_hbm.shape[0]
     choices = ids_hbm.shape[0]
@@ -103,6 +103,23 @@
            pltpu.make_async_copy(tok_hbm, xg.at[my_rows], in_sem.at[2])]
     for c in own:
         c.start()
+
+    pairs = (tp + 1 - 2 * parity, y_target(tp_n - 1 + 2 * parity))
+
+    def span(u):
+        return pl.ds(u * unit, unit)
+
+    def mine(u):
+        return pl.ds(pl.multiple_of(u * unit + parity * LANES, LANES), LANES)
+
+    def theirs(u):
+        return pl.ds(pl.multiple_of(u * unit + (1 - parity) * LANES, LANES), LANES)
+
+    def packed(u):
+        return pl.ds(u * LANES, LANES)
+
+    for u in range(STRAIGHT):
+        zr[far_slots, theirs(u)] = jnp.zeros((2 * cap, LANES), F32)
 
     bar = pltpu.get_barrier_semaphore()
     for dt in range(1, tp_n):
@@ -231,20 +248,7 @@
         lax.fori_loop(0, local, up, 0, unroll=True)
 
     arrived(wd, w_sem.at[2])
-    pairs = (tp + 1 - 2 * parity, y_target(tp_n - 1 + 2 * parity))
     group = slots // 2
-
-    def span(u):
-        return pl.ds(u * unit, unit)
-
-    def mine(u):
-        return pl.ds(pl.multiple_of(u * unit + parity * LANES, LANES), LANES)
-
-    def theirs(u):
-        return pl.ds(pl.multiple_of(u * unit + (1 - parity) * LANES, LANES), LANES)
-
-    def packed(u):
-        return pl.ds((u - STRAIGHT) * LANES, LANES)
 
     def down(u):
         cols = span(u)
@@ -254,26 +258,40 @@
             total = o if total is None else total + o
         ob[:, cols] = total
         if u < STRAIGHT:
-            for p in x_peers:
+            for p in near:
                 to = x_target(p)
                 send(ob.at[slots_of(to), cols], zr.at[my_slots, cols], out_sem.at[5], cx_rs.at[u], device(to, tp))
+            for p, to in zip(far, pairs):
+                part = slots_of(x_target(p))
+                send(ob.at[part, theirs(u)], pr.at[part, packed(u)], out_sem.at[8], pr_rs.at[u], device(ep, to))
             zr[my_slots, cols] = ob[my_slots, cols]
         else:
             for g, to in enumerate(pairs):
                 part = pl.ds(g * group, group)
                 send(ob.at[part, theirs(u)], pr.at[part, packed(u)], out_sem.at[6], pr_rs.at[u], device(ep, to))
 
+    def far_sum(u):
+        arrived(pr.at[pl.ds(0, 2 * cap), packed(u)], pr_rs.at[u])
+        for p in far:
+            to = x_target(p)
+            zs[slots_of(to), packed(u)] = ob[slots_of(to), mine(u)] + pr[slots_of(to), packed(u)]
+            send(zs.at[slots_of(to), packed(u)], zr.at[my_slots, mine(u)], out_sem.at[9], cf_rs.at[u], device(to, tp))
+
     def pair_sum(u):
         arrived(pr.at[:, packed(u)], pr_rs.at[u])
         zs[:, packed(u)] = ob[:, mine(u)] + pr[:, packed(u)]
         for p in x_peers:
             to = x_target(p)
-            send(zs.at[slots_of(to), packed(u)], zr.at[my_slots, mine(u)], out_sem.at[5], cx_rs.at[u], device(to, tp))
+            send(zs.at[slots_of(to), packed(u)], zr.at[my_slots, mine(u)], out_sem.at[10], cx_rs.at[u], device(to, tp))
         zr[my_slots, mine(u)] = zs[my_slots, packed(u)]
 
     def combine(u):
-        cols, width = (span(u), unit) if u < STRAIGHT else (mine(u), LANES)
-        arrived(zr.at[pl.ds(0, len(x_peers) * cap), pl.ds(0, width)], cx_rs.at[u])
+        cols = span(u) if u < STRAIGHT else mine(u)
+        if u < STRAIGHT:
+            arrived(zr.at[near_rows, pl.ds(0, unit)], cx_rs.at[u])
+            arrived(zr.at[pl.ds(0, 2 * cap), pl.ds(0, LANES)], cf_rs.at[u])
+        else:
+            arrived(zr.at[pl.ds(0, len(x_peers) * cap), pl.ds(0, LANES)], cx_rs.at[u])
         z1, z2, z3 = split3(zr[:, cols])
         pick = row_of[...]
         yb[:, cols] = dot(pick, z3) + dot(pick, z2) + dot(pick, z1)
@@ -293,9 +311,9 @@
 
     for u in (0, 2, 3, 1, 4, 5, 6, 7):
         down(u)
-    for step, u in ((pair_sum, 2), (pair_sum, 3), (combine, 0), (pair_sum, 4), (pair_sum, 5), (combine, 1),
-                    (pair_sum, 6), (combine, 2), (pair_sum, 7), (combine, 3), (combine, 4), (combine, 5),
-                    (combine, 6), (combine, 7)):
+    for step, u in ((far_sum, 0), (pair_sum, 2), (pair_sum, 3), (far_sum, 1), (combine, 0), (pair_sum, 4),
+                    (pair_sum, 5), (combine, 1), (pair_sum, 6), (combine, 2), (pair_sum, 7), (combine, 3),
+                    (combine, 4), (combine, 5), (combine, 6), (combine, 7)):
         step(u)
     for u in range(units):
         finish(u)
@@ -309,8 +327,11 @@
     arrived(xs.at[pl.ds(0, others * 2 * cap), pl.ds(0, kw)], out_sem.at[4])
     paired = units - STRAIGHT
     sent = pl.ds(0, STRAIGHT * unit + paired * LANES)
-    arrived(ob.at[pl.ds(0, len(x_peers) * cap), sent], out_sem.at[5])
-    arrived(pr, out_sem.at[6])
+    arrived(ob.at[near_rows, pl.ds(0, STRAIGHT * unit)], out_sem.at[5])
+    arrived(pr.at[:, pl.ds(0, paired * LANES)], out_sem.at[6])
+    arrived(pr.at[pl.ds(0, 2 * cap), pl.ds(0, STRAIGHT * LANES)], out_sem.at[8])
+    arrived(pr.at[pl.ds(0, 2 * cap), pl.ds(0, STRAIGHT * LANES)], out_sem.at[9])
+    arrived(ob.at[pl.ds(0, len(x_peers) * cap), pl.ds(0, paired * LANES)], out_sem.at[10])
     arrived(yr.at[:, :, sent], out_sem.at[7])
 
 
@@ -354,13 +375,13 @@
                 pltpu.VMEM((slots, d), F32),
                 pltpu.VMEM((shard_rows, d), F32),
                 pltpu.VMEM((ny, rows, d), F32),
-                pltpu.VMEM((slots, d // 2 - STRAIGHT * LANES), F32),
-                pltpu.VMEM((slots, d // 2 - STRAIGHT * LANES), F32),
+                pltpu.VMEM((slots, d // 2), F32),
+                pltpu.VMEM((slots, d // 2), F32),
                 pltpu.VMEM((slots, shard_rows), BF16),
                 pltpu.VMEM((shard_rows, slots), BF16),
                 pltpu.VMEM((LANES, LANES), F32),
                 dma((3,)), dma((3,)), dma((4,)), dma((CHUNKS + 1,)), dma((1,)), dma((2,)), dma((CHUNKS,)), dma((ny,)),
-                dma((units,)), dma((units,)), dma((units,)), dma((8,)),
+                dma((units,)), dma((units,)), dma((STRAIGHT,)), dma((units,)), dma((11,)),
             ],
             compiler_params=pltpu.CompilerParams(collective_id=0, has_side_effects=True,
                                                  vmem_limit_bytes=60 * 1024 * 1024),

time: 44.4 us -> 45.3 us (1.020)
  Pallas kernels: 43.6 us -> 44.6 us
    pallas_call x1, Pallas kernels: 43.6 us -> 44.6 us  [block(): pl.pallas_call(functools.partial(moe_kernel, names, ep_n, tp_n), out_shap...]
where the time goes in v13:
time: 45.3 us
  Pallas kernels  44.6 us (98%)
  local copies, waits for them, and re-layouts  0.66 us (1%)
    pallas_call x1, Pallas kernels, block(): pl.pallas_call(functools.partial(moe_kernel, names, ep_n, tp_n), out_shap...  44.6 us

profile of v13, /device:TPU:97, one launch (start us, length us, event | category | flops | bytes accessed | tf_op | source)
XLA Modules:
  0.0 45.3 jit_solution(5409969636838076010)
XLA Ops:
  0.0 44.6 %shard_map.64 = bf16[32,2048]{1,0:T(8,128)(2,1)S(1)} custom-call(bf16[32,2048]{1,0:T(8,128)(2,1)} %tok_hbm.1, s32[8,32]{1,0:T(8,128)} %bitcast.2, f32[8,32]{1,0:T(8,128)} %bitcast.3, bf16[8,2048,256]{2,1,0:T(8,128)(2,1)} %wg_hbm.1, bf16[8,2048,256]{2,1,0:T(8,128)(2,1)} %wu_hbm.1, bf16[8,256,2048]{2,1,0:T(8,128)(2,1)} %wd_hbm.1), custom_call_target="tpu_custom_call" | custom-call | tf_op jit(solution)/shard_map/pallas_call | solution.py:354
  44.6 0.7 %copy.8 = bf16[32,2048]{1,0:T(8,128)(2,1)} copy(bf16[32,2048]{1,0:T(8,128)(2,1)S(1)} %shard_map.64) | data formatting | bytes 262144
